TPU v7x, 32 devices: a whole 2x2x4 slice. The times are simulated.
32 devices in a mesh: dp: 32 (over z, y, x, core), tensor: 1.
Axes of the slice: x: 2, y: 2, z: 4, core: 2. Of those that a mesh axis runs over, the one named last changes fastest.
Arguments:
- tokens: bfloat16 [4096, 2048], P('dp'), may hold values from -8 to 8
- grad_out: bfloat16 [4096, 2048], P('dp'), may hold values from -6 to 6
- route_ids: int32 [4096, 4], P('dp'), may hold values from 0 to 59, as said below
- expert_map: int32 [60], replicated, may hold values from 0 to 63, as said below
- router: bfloat16 [2048, 60], replicated, may hold values from -1 to 1
- shared_gate: bfloat16 [2048], replicated, may hold values from -0.125 to 0.125
- sh_gate: bfloat16 [2048, 2816], P('dp', 'tensor'), may hold values from -0.125 to 0.125
- sh_up: bfloat16 [2048, 2816], P('dp', 'tensor'), may hold values from -0.125 to 0.125
- sh_down: bfloat16 [2816, 2048], P('tensor', 'dp'), may hold values from -0.109375 to 0.109375
- ex_gate: bfloat16 [64, 2048, 1408], P('dp', None, 'tensor'), may hold values from -0.125 to 0.125
- ex_up: bfloat16 [64, 2048, 1408], P('dp', None, 'tensor'), may hold values from -0.125 to 0.125
- ex_down: bfloat16 [64, 1408, 2048], P('dp', 'tensor'), may hold values from -0.15625 to 0.15625
Outputs:
- mixed: bfloat16 [4096, 2048], P('dp', 'tensor')
- grad_tokens: bfloat16 [4096, 2048], P('dp', 'tensor')
Inputs may be any that keep to these rules, and one draw needn't show every extreme that they name: `route_ids`: each row names 4 different experts. Within the rows of one device (aligned blocks of 128 rows), no expert is named more than 9 times over all 4 columns, and some expert is named exactly 9 times. Entries are distinct. Expert e uses the weights of slot expert_map[e]; slot s is held by index s // 2 of dp. Slots that no expert names are not used.
All inputs are finite; a program needn't handle non-finite values.
Results may differ from a plain program's by a relative error of at most 0.011.
Values may be sent and summed in bfloat16 or wider, within the bound.
No kernel may reach another device: no remote copies, remote signals or barrier semaphores. Data moves between devices by JAX's collectives and lax.ppermute only.
A program may use at most 128 MiB of HBM per device.

v0:
```python
import jax
import jax.numpy as jnp
from jax import lax
from jax.experimental import pallas as pl
from jax.experimental.pallas import tpu as pltpu
from jax.sharding import PartitionSpec as P


CAP = 9


def silu_pair(pre_gate):
    sigmoid_val = 1.0 / (1.0 + jnp.exp(-pre_gate))
    return (pre_gate * sigmoid_val, sigmoid_val * (1.0 + pre_gate * (1.0 - sigmoid_val)))


def contract_last(left, right):
    return lax.dot_general(
        left, right, (((1,), (1,)), ((), ())), preferred_element_type=jnp.float32
    )


def expert_block(rows_in, rows_cot, w_gate, w_up, w_down):
    pre_gate = jnp.dot(rows_in, w_gate, preferred_element_type=jnp.float32)
    pre_up = jnp.dot(rows_in, w_up, preferred_element_type=jnp.float32)
    active, derivative = silu_pair(pre_gate)
    hidden = (active * pre_up).astype(jnp.bfloat16)
    result = jnp.dot(hidden, w_down, preferred_element_type=jnp.float32)
    grad_hidden = contract_last(rows_cot, w_down)
    grad_gate = (grad_hidden * pre_up * derivative).astype(jnp.bfloat16)
    grad_up = (grad_hidden * active).astype(jnp.bfloat16)
    backward = contract_last(grad_gate, w_gate) + contract_last(grad_up, w_up)
    return (result, backward)


def expert_batch(rows_in, rows_cot, w_gate, w_up, w_down):
    pre_gate = jnp.einsum("slcd,ldf->slcf", rows_in, w_gate, preferred_element_type=jnp.float32)
    pre_up = jnp.einsum("slcd,ldf->slcf", rows_in, w_up, preferred_element_type=jnp.float32)
    active, derivative = silu_pair(pre_gate)
    hidden = (active * pre_up).astype(jnp.bfloat16)
    result = jnp.einsum(
        "slcf,lfd->slcd", hidden, w_down, preferred_element_type=jnp.float32
    ).astype(jnp.bfloat16)
    grad_hidden = jnp.einsum("slcd,lfd->slcf", rows_cot, w_down, preferred_element_type=jnp.float32)
    grad_gate = (grad_hidden * pre_up * derivative).astype(jnp.bfloat16)
    grad_up = (grad_hidden * active).astype(jnp.bfloat16)
    grad_both = jnp.concatenate([grad_gate, grad_up], axis=3)
    weight_both = jnp.concatenate([w_gate, w_up], axis=2)
    backward = jnp.einsum(
        "slcf,ldf->slcd", grad_both, weight_both, preferred_element_type=jnp.float32
    )
    return (result, backward.astype(jnp.bfloat16))


def shards(
    tokens,
    grad_out,
    route_ids,
    expert_map,
    router,
    shared_gate,
    sh_gate,
    sh_up,
    sh_down,
    ex_gate,
    ex_up,
    ex_down,
):
    tok_dev, width = tokens.shape
    top_count = route_ids.shape[1]
    expert_count = router.shape[1]
    dp_size = lax.axis_size("dp")
    tensor_size = lax.axis_size("tensor")
    tensor_rank = lax.axis_index("tensor")
    local_slots = ex_gate.shape[0]
    col_width = width // tensor_size
    col_start = tensor_rank * col_width
    buffer_rows = dp_size * local_slots * CAP
    slot_rows = local_slots * CAP
    flat_ids = route_ids.reshape(-1)
    chosen = (flat_ids[:, None] == jnp.arange(expert_count, dtype=jnp.int32)[None, :]).astype(
        jnp.int32
    )
    earlier = jnp.sum((jnp.cumsum(chosen, axis=0) - chosen) * chosen, axis=1)
    slot_of = jnp.sum(chosen * expert_map[None, :], axis=1)
    position = slot_of * CAP + earlier
    token_index = jnp.arange(tok_dev * top_count, dtype=jnp.int32) // top_count
    source_rows = jnp.full((buffer_rows,), tok_dev, jnp.int32).at[position].set(token_index)

    def fetch_rows(table):
        padded = jnp.concatenate([table, jnp.zeros((1, table.shape[1]), table.dtype)], axis=0)
        return jnp.take(padded, source_rows, axis=0)

    send_in = fetch_rows(tokens).reshape(dp_size, slot_rows, width)
    send_cot = fetch_rows(grad_out).reshape(dp_size, slot_rows, width)
    got_in = lax.all_to_all(send_in, "dp", split_axis=0, concat_axis=0, tiled=True)
    got_cot = lax.all_to_all(send_cot, "dp", split_axis=0, concat_axis=0, tiled=True)
    grid_shape = (dp_size, local_slots, CAP, width)
    result, backward = expert_batch(
        got_in.reshape(grid_shape), got_cot.reshape(grid_shape), ex_gate, ex_up, ex_down
    )
    came_out = lax.all_to_all(
        result.reshape(dp_size, slot_rows, width), "dp", split_axis=0, concat_axis=0, tiled=True
    )
    came_back = lax.all_to_all(
        backward.reshape(dp_size, slot_rows, width), "dp", split_axis=0, concat_axis=0, tiled=True
    )
    routed_out = came_out.reshape(buffer_rows, width)
    routed_back = came_back.reshape(buffer_rows, width)
    weights = (
        lax.all_gather(sh_gate, "dp", axis=0, tiled=True),
        lax.all_gather(sh_up, "dp", axis=0, tiled=True),
        lax.all_gather(sh_down, "dp", axis=1, tiled=True),
    )
    full_gate, full_up, full_down = weights
    sh_out, sh_back = expert_block(tokens, grad_out, full_gate, full_up, full_down)
    routed_width = routed_out.shape[1]
    expert_out = jnp.take(routed_out, position, axis=0).reshape(tok_dev, top_count, routed_width)
    expert_back = jnp.take(routed_back, position, axis=0).reshape(tok_dev, top_count, routed_width)
    logits = jnp.dot(tokens, router, preferred_element_type=jnp.float32)
    exp_logit = jnp.exp(logits)
    prob_table = exp_logit / jnp.sum(exp_logit, axis=1, keepdims=True)
    picked = chosen.reshape(tok_dev, top_count, expert_count).astype(jnp.float32)
    gate_weights = jnp.sum(picked * prob_table[:, None, :], axis=2)
    shared_scale = 1.0 / (
        1.0 + jnp.exp(-jnp.dot(tokens, shared_gate, preferred_element_type=jnp.float32))
    )
    shared_part = jnp.sum(grad_out.astype(jnp.float32) * sh_out, axis=1)
    dots_part = jnp.einsum("td,tkd->tk", grad_out, expert_out, preferred_element_type=jnp.float32)
    mixed_part = (
        jnp.sum(gate_weights[:, :, None] * expert_out.astype(jnp.float32), axis=1)
        + shared_scale[:, None] * sh_out
    )
    grad_part = (
        jnp.sum(gate_weights[:, :, None] * expert_back.astype(jnp.float32), axis=1)
        + shared_scale[:, None] * sh_back
    )
    out_dots, shared_dots = lax.psum((dots_part, shared_part), "tensor")
    mixed_cols, grad_cols = (
        lax.psum_scatter(mixed_part, "tensor", scatter_dimension=1, tiled=True),
        lax.psum_scatter(grad_part, "tensor", scatter_dimension=1, tiled=True),
    )
    grad_prob = jnp.sum(picked * out_dots[:, :, None], axis=1)
    dlogits = prob_table * (grad_prob - jnp.sum(gate_weights * out_dots, axis=1, keepdims=True))
    router_cols = lax.dynamic_slice_in_dim(router, col_start, col_width, 0).astype(jnp.float32)
    grad_router = lax.dot_general(
        dlogits,
        router_cols,
        (((1,), (1,)), ((), ())),
        precision=lax.Precision.HIGHEST,
        preferred_element_type=jnp.float32,
    )
    gate_cols = lax.dynamic_slice_in_dim(shared_gate, col_start, col_width, 0).astype(jnp.float32)
    slope_term = shared_dots * shared_scale * (1.0 - shared_scale)
    grad_total = grad_cols + grad_router + slope_term[:, None] * gate_cols[None, :]
    return (mixed_cols.astype(jnp.bfloat16), grad_total.astype(jnp.bfloat16))


def dot32(left, right):
    return jnp.dot(left, right, preferred_element_type=jnp.float32)


def expert_hidden(rows_in, w_gate, w_up):
    pre_gate = jnp.einsum("slcd,ldf->slcf", rows_in, w_gate, preferred_element_type=jnp.float32)
    pre_up = jnp.einsum("slcd,ldf->slcf", rows_in, w_up, preferred_element_type=jnp.float32)
    return pre_gate, pre_up


def assemble_kernel(order_ref, stacks, targets):
    first = 0
    for source, low in stacks:
        blocks, _, rows, _ = source.shape
        for j in range(blocks):
            for w, target in enumerate(targets):
                target[order_ref[first + j], low : low + rows, :] = source[j, w]
        first += blocks


def assemble(order, stacks, lows, shape):
    def kernel(order_ref, *refs):
        assemble_kernel(order_ref, list(zip(refs[:-3], lows)), refs[-3:])

    size = 3 * 2 * shape[0] * shape[1] * shape[2]
    return pl.pallas_call(
        kernel,
        in_specs=[pl.BlockSpec(memory_space=pltpu.SMEM)]
        + [pl.BlockSpec(memory_space=pltpu.VMEM)] * len(stacks),
        out_specs=[pl.BlockSpec(memory_space=pltpu.VMEM)] * 3,
        out_shape=[jax.ShapeDtypeStruct(shape, stacks[0].dtype)] * 3,
        cost_estimate=pl.CostEstimate(
            flops=100 * size, bytes_accessed=2 * size, transcendentals=0
        ),
    )(order, *stacks)


def after(value, *others):
    return lax.optimization_barrier((value,) + others)[0]


def paired_shards(
    tokens,
    grad_out,
    route_ids,
    expert_map,
    router,
    shared_gate,
    sh_gate,
    sh_up,
    sh_down,
    ex_gate,
    ex_up,
    ex_down,
):
    tok_dev, width = tokens.shape
    top_count = route_ids.shape[1]
    expert_count = router.shape[1]
    dp_size = lax.axis_size("dp")
    local_slots = ex_gate.shape[0]
    half_size = dp_size // 2
    lanes = half_size // 2
    lane_bits = lanes.bit_length() - 1
    rows_slot = -(-4 * CAP // 8) * 8
    rows_all = lanes * local_slots * rows_slot
    me = lax.axis_index("dp")
    half = me // half_size
    lane = (me % half_size) // 2
    core = me % 2
    pair_half = [(i, i ^ half_size) for i in range(dp_size)]
    pair_core = [(i, i ^ 1) for i in range(dp_size)]
    lane_groups = [
        [h * half_size + 2 * n + c for n in range(lanes)] for h in range(2) for c in range(2)
    ]

    def across(value, pairs):
        return lax.ppermute(value, "dp", pairs)

    def exchange(value):
        return lax.all_to_all(
            value, "dp", split_axis=0, concat_axis=0, tiled=True, axis_index_groups=lane_groups
        )

    tokens_far = across(tokens, pair_half)
    grads_far = across(after(grad_out, tokens_far), pair_half)
    tokens_two = jnp.concatenate([tokens, tokens_far], axis=0)
    grads_two = jnp.concatenate([grad_out, grads_far], axis=0)

    chosen = (
        route_ids[:, :, None] == jnp.arange(expert_count, dtype=jnp.int32)[None, None, :]
    ).astype(jnp.float32)
    named = jnp.sum(chosen, axis=1)
    before = (
        jnp.arange(tok_dev, dtype=jnp.int32)[:, None]
        > jnp.arange(tok_dev, dtype=jnp.int32)[None, :]
    ).astype(jnp.bfloat16)
    earlier = dot32(before, named.astype(jnp.bfloat16))
    rank = jnp.sum(chosen * earlier[:, None, :], axis=2)
    slot = jnp.sum(chosen * expert_map.astype(jnp.float32)[None, None, :], axis=2)
    logits = dot32(tokens, router)
    exp_logit = jnp.exp(logits)
    prob_table = exp_logit / jnp.sum(exp_logit, axis=1, keepdims=True)
    gate_weights = jnp.sum(chosen * prob_table[:, None, :], axis=2)
    shared_scale = 1.0 / (1.0 + jnp.exp(-dot32(tokens, shared_gate)))
    meta = jnp.concatenate([slot, rank, gate_weights, shared_scale[:, None]], axis=1)
    meta_two = jnp.concatenate([meta, across(meta, pair_half)], axis=0)
    meta_all = jnp.concatenate([meta_two, across(meta_two, pair_core)], axis=0)
    tokens_all = jnp.concatenate([tokens_two, across(tokens_two, pair_core)], axis=0)
    grads_all = jnp.concatenate([grads_two, across(grads_two, pair_core)], axis=0)
    tok_all = 4 * tok_dev

    slot_all = meta_all[:, :top_count].astype(jnp.int32)
    rank_all = meta_all[:, top_count : 2 * top_count].astype(jnp.int32)
    gates_all = meta_all[:, 2 * top_count : 3 * top_count]
    scale_all = meta_all[:, 3 * top_count :]
    holder = slot_all // local_slots
    block = jnp.arange(tok_all, dtype=jnp.int32)[:, None] // tok_dev
    row_at = ((holder % half_size) // 2) * local_slots + slot_all % local_slots
    row_at = row_at * rows_slot + block * CAP + rank_all
    row_at = jnp.where((holder // half_size == half) & (holder % 2 == core), row_at, -1)
    row_ids = jnp.arange(rows_all, dtype=jnp.int32)
    pick_rows = jnp.sum(
        (row_at.T[:, None, :] == row_ids[None, :, None]).astype(jnp.float32), axis=0
    ).astype(jnp.bfloat16)
    hit = row_at[:, :, None] == row_ids[None, None, :]
    place = jnp.sum(jnp.where(hit, gates_all[:, :, None], 0.0), axis=1).astype(jnp.bfloat16)

    def dispatch(table):
        rows = dot32(pick_rows, table).astype(jnp.bfloat16)
        got = exchange(rows.reshape(lanes, local_slots * rows_slot, width))
        return got.reshape(lanes, local_slots, rows_slot, width)

    def give_back(rows):
        sent = rows.reshape(lanes, local_slots * rows_slot, width)
        return exchange(sent).reshape(rows_all, width)

    got_in = dispatch(tokens_all)
    got_cot = dispatch(grads_all)

    hidden_all = sh_gate.shape[1]
    quarter = hidden_all // 4
    quarter_pad = -(-quarter // 128) * 128
    shard = jnp.stack([sh_gate, sh_up, sh_down.T]).reshape(3, width // dp_size, 4, quarter)
    shard = jnp.pad(shard, ((0, 0), (0, 0), (0, 0), (0, quarter_pad - quarter)))
    shard = shard.transpose(2, 0, 1, 3).reshape(2, 2, 3, width // dp_size, quarter_pad)
    kept = lax.dynamic_index_in_dim(shard, core, 0, keepdims=False)
    sent = lax.dynamic_index_in_dim(shard, 1 - core, 0, keepdims=False)
    came = across(sent, pair_core)
    both = jnp.where(
        core == 0, jnp.concatenate([kept, came], axis=2), jnp.concatenate([came, kept], axis=2)
    )
    own_rows = lax.dynamic_index_in_dim(both, half, 0, keepdims=False)
    far_rows = lax.dynamic_index_in_dim(both, 1 - half, 0, keepdims=False)
    far_rows = across(after(far_rows, grads_far), pair_half)

    def lane_hop(value, bit):
        return across(value, [(i, i ^ (2 * bit)) for i in range(dp_size)])

    def spread(block):
        top = lanes // 2
        held_all = jnp.stack([block, lane_hop(block, top)])
        chains = max(lane_bits - 1, 1)
        rows = block.shape[1] // chains
        stacks, lows, sources = [], [], []
        for chain in range(chains):
            held, came_from = held_all[:, :, chain * rows : (chain + 1) * rows], [0, top]
            bits = [1 << ((chain + step) % chains) for step in range(lane_bits - 1)]
            for step, bit in enumerate(bits):
                received = lane_hop(held, bit)
                moved = [d ^ bit for d in came_from]
                if step == len(bits) - 1:
                    stacks += [held, received]
                    lows += [chain * rows] * 2
                    sources += came_from + moved
                else:
                    held = jnp.concatenate([held, received], axis=0)
                    came_from = came_from + moved
        return stacks, lows, sources

    pre_gate, pre_up = expert_hidden(got_in, ex_gate, ex_up)
    active, derivative = silu_pair(pre_gate)
    hidden = (active * pre_up).astype(jnp.bfloat16)
    result = jnp.einsum(
        "slcf,lfd->slcd", hidden, ex_down, preferred_element_type=jnp.float32
    ).astype(jnp.bfloat16)
    routed_out = give_back(result)
    grad_hidden = jnp.einsum("slcd,lfd->slcf", got_cot, ex_down, preferred_element_type=jnp.float32)
    grad_gate = (grad_hidden * pre_up * derivative).astype(jnp.bfloat16)
    grad_up = (grad_hidden * active).astype(jnp.bfloat16)
    grad_both = jnp.concatenate([grad_gate, grad_up], axis=3)
    weight_both = jnp.concatenate([ex_gate, ex_up], axis=2)
    backward = jnp.einsum(
        "slcf,ldf->slcd", grad_both, weight_both, preferred_element_type=jnp.float32
    ).astype(jnp.bfloat16)
    routed_back = give_back(backward)

    own_stacks, own_lows, sources = spread(own_rows)
    far_stacks, far_lows, _ = spread(far_rows)
    lanes_of = jnp.array(sources, jnp.int32) ^ lane
    order = jnp.concatenate([half * lanes + lanes_of, (1 - half) * lanes + lanes_of])
    full = assemble(
        order,
        own_stacks + far_stacks,
        own_lows + far_lows,
        (2 * lanes, own_rows.shape[1], quarter_pad),
    )
    full_gate, full_up, full_down = [f.reshape(width, quarter_pad) for f in full]

    sh_pre_gate = dot32(tokens_all, full_gate)
    sh_pre_up = dot32(tokens_all, full_up)
    sh_active, sh_derivative = silu_pair(sh_pre_gate)
    sh_hidden = (sh_active * sh_pre_up).astype(jnp.bfloat16)
    sh_out = contract_last(sh_hidden, full_down)
    mixed_part = dot32(place, routed_out) + scale_all * sh_out
    sh_grad_hidden = dot32(grads_all, full_down)
    sh_grad_gate = (sh_grad_hidden * sh_pre_up * sh_derivative).astype(jnp.bfloat16)
    sh_grad_up = (sh_grad_hidden * sh_active).astype(jnp.bfloat16)
    sh_back = contract_last(sh_grad_gate, full_gate) + contract_last(sh_grad_up, full_up)
    sh_back = lax.optimization_barrier(scale_all * sh_back)

    def collect(partial):
        sent = partial[2 * tok_dev :].astype(jnp.bfloat16)
        came = across(sent, pair_core).astype(jnp.float32)
        pair_sum = partial[: 2 * tok_dev] + came
        sent = pair_sum[tok_dev:].astype(jnp.bfloat16)
        return pair_sum[:tok_dev] + across(sent, pair_half).astype(jnp.float32)

    mixed = collect(mixed_part)
    all_dots = contract_last(grads_all, routed_out)
    dots_part = jnp.sum(jnp.where(hit, all_dots[:, None, :], 0.0), axis=2)
    shared_part = jnp.sum(grads_all.astype(jnp.float32) * sh_out, axis=1, keepdims=True)
    scalars = jnp.concatenate([dots_part, shared_part], axis=1)
    scalars = scalars[: 2 * tok_dev] + across(scalars[2 * tok_dev :], pair_core)
    scalars = scalars[:tok_dev] + across(scalars[tok_dev:], pair_half)
    out_dots = scalars[:, :top_count]
    shared_dots = scalars[:, top_count]
    grad_part = collect(dot32(place, routed_back) + sh_back)

    grad_prob = jnp.sum(chosen * out_dots[:, :, None], axis=1)
    dlogits = prob_table * (grad_prob - jnp.sum(gate_weights * out_dots, axis=1, keepdims=True))
    grad_router = lax.dot_general(
        dlogits,
        router.astype(jnp.float32),
        (((1,), (1,)), ((), ())),
        precision=lax.Precision.HIGHEST,
        preferred_element_type=jnp.float32,
    )
    slope_term = shared_dots * shared_scale * (1.0 - shared_scale)
    grad_total = (
        grad_part + grad_router + slope_term[:, None] * shared_gate.astype(jnp.float32)[None, :]
    )
    return (mixed.astype(jnp.bfloat16), grad_total.astype(jnp.bfloat16))


def solution(mesh):
    dp_size = mesh.shape["dp"]
    paired = mesh.shape["tensor"] == 1 and dp_size >= 8 and dp_size & (dp_size - 1) == 0
    placed = (
        P("dp", None),
        P("dp", None),
        P("dp", None),
        P(),
        P(),
        P(),
        P("dp", "tensor"),
        P("dp", "tensor"),
        P("tensor", "dp"),
        P("dp", None, "tensor"),
        P("dp", None, "tensor"),
        P("dp", "tensor", None),
    )

    def body(*operands):
        return (paired_shards if paired else shards)(*operands)

    return jax.shard_map(
        body,
        mesh=mesh,
        in_specs=placed,
        out_specs=(P("dp", "tensor"), P("dp", "tensor")),
        check_vma=False,
    )
```

profile of v0, /device:TPU:0, one launch (start us, length us, event | category | flops | bytes accessed | tf_op | source)
XLA Modules:
  0.0 389.7 jit_solution(14659204927292663582)
XLA Ops:
  0.7 4.1 %collective-permute-start.2 = (bf16[128,2048]{1,0:T(8,128)(2,1)}, bf16[128,2048]{1,0:T(8,128)(2,1)S(1)}, u32[]{:S(2)}, u32[]{:S(2)}) collective-permute-start(bf16[128,2048]{1,0:T(8,128)(2,1)} %param.13), channel_id=1, source_target_pairs={{0,16},{1,17},{2,18},{3,19},{4,20},{5,21},{6,22},{7,23},{8,24},{9,... | collective-permute-start | bytes 1572872 | tf_op jit(solution)/shard_map/ppermute | solution.py:235
  10.8 17.7 %collective-permute-done.2 = bf16[128,2048]{1,0:T(8,128)(2,1)S(1)} collective-permute-done((bf16[128,2048]{1,0:T(8,128)(2,1)}, bf16[128,2048]{1,0:T(8,128)(2,1)S(1)}, u32[]{:S(2)}, u32[]{:S(2)}) %collective-permute-start.2) | collective-permute-done | bytes 524320 | tf_op jit(solution)/shard_map/ppermute | solution.py:235
  35.2 4.6 %convolution_convert_fusion.1 = bf16[640,2048]{1,0:T(8,128)(2,1)} fusion(bf16[512,2048]{1,0:T(8,128)(2,1)} %constant_dynamic-update-slice_fusion, bf16[640,512]{1,0:T(8,128)(2,1)S(1)} %convert_reduce_fusion), kind=kOutput, calls=%fused_computation.41 | convolution fusion | flops 1343488000 | bytes 5373952 | tf_op jit(solution)/shard_map/dot_general | solution.py:160
  39.8 4.6 %all-to-all-start = ((bf16[8,80,2048]{2,1,0:T(8,128)(2,1)}), bf16[8,80,2048]{2,1,0:T(8,128)(2,1)}, u32[]{:S(2)}, u32[]{:S(2)}) async-start(bf16[8,80,2048]{2,1,0:T(8,128)(2,1)} %bitcast.3), calls=%async_computation | async-start | bytes 5242880 | tf_op jit(solution)/shard_map/all_to_all | solution.py:238
  45.8 2.9 collective-permute-start.10
  50.4 34.1 %collective-permute-done.10 = bf16[128,2048]{1,0:T(8,128)(2,1)} collective-permute-done((bf16[128,2048]{1,0:T(8,128)(2,1)S(1)}, bf16[128,2048]{1,0:T(8,128)(2,1)}, u32[]{:S(2)}, u32[]{:S(2)}) %collective-permute-start.10) | collective-permute-done | bytes 524320 | tf_op jit(solution)/shard_map/ppermute | solution.py:235
  84.5 2.1 pad_maximum_fusion.5
  87.2 1.6 maximum_select_fusion
  89.0 3.6 collective-permute-start.11
  92.6 1.5 collective-permute-start.5
  95.2 24.2 %collective-permute-done.11 = bf16[3,128,768]{2,1,0:T(8,128)(2,1)} collective-permute-done((bf16[3,128,768]{2,1,0:T(8,128)(2,1)S(1)}, bf16[3,128,768]{2,1,0:T(8,128)(2,1)}, u32[]{:S(2)}, u32[]{:S(2)}) %collective-permute-start.11) | collective-permute-done | bytes 589856 | tf_op jit(solution)/shard_map/ppermute | solution.py:235
  121.3 3.1 convolution_convert_fusion
  124.4 9.4 %all-to-all-start.2 = ((bf16[8,80,2048]{2,1,0:T(8,128)(2,1)}), bf16[8,80,2048]{2,1,0:T(8,128)(2,1)S(1)}, u32[]{:S(2)}, u32[]{:S(2)}) async-start(bf16[8,80,2048]{2,1,0:T(8,128)(2,1)} %bitcast.149), calls=%async_computation.2 | async-start | bytes 5242880 | tf_op jit(solution)/shard_map/all_to_all | solution.py:238
  135.0 2.1 collective-permute-start.6
  141.1 3.4 collective-permute-start.13
  144.6 33.8 %collective-permute-done.6 = bf16[2,3,64,768]{3,2,1,0:T(8,128)(2,1)S(1)} collective-permute-done((bf16[2,3,64,768]{3,2,1,0:T(8,128)(2,1)S(1)}, bf16[2,3,64,768]{3,2,1,0:T(8,128)(2,1)S(1)}, u32[]{:S(2)}, u32[]{:S(2)}) %collective-permute-start.6) | collective-permute-done | bytes 589856 | tf_op jit(solution)/shard_map/ppermute | solution.py:235
  183.1 8.0 %collective-permute-done.13 = bf16[2,3,64,768]{3,2,1,0:T(8,128)(2,1)S(1)} collective-permute-done((bf16[2,3,64,768]{3,2,1,0:T(8,128)(2,1)S(1)}, bf16[2,3,64,768]{3,2,1,0:T(8,128)(2,1)S(1)}, u32[]{:S(2)}, u32[]{:S(2)}) %collective-permute-start.13) | collective-permute-done | bytes 589856 | tf_op jit(solution)/shard_map/ppermute | solution.py:235
  192.2 1.5 collective-permute-start.14
  195.7 11.2 %fusion.3 = f32[2,8,40,1408]{3,2,1,0:T(8,128)} fusion(bf16[2,2048,1408]{2,1,0:T(8,128)(2,1)} %param.23, bf16[8,2,40,2048]{3,2,1,0:T(8,128)(2,1)} %bitcast.4), kind=kOutput, calls=%fused_computation.4 | convolution fusion | flops 3690987520 | bytes 17760256 | tf_op jit(solution)/shard_map/slcd,ldf->slcf/dot_general | solution.py:165
  207.0 8.0 %fusion.5 = f32[2,8,40,1408]{3,2,1,0:T(8,128)} fusion(bf16[2,2048,1408]{2,1,0:T(8,128)(2,1)S(1)} %bitcast.163, bf16[8,2,40,2048]{3,2,1,0:T(8,128)(2,1)} %bitcast.4), kind=kOutput, calls=%fused_computation.6 | convolution fusion | flops 3690987520 | bytes 17760256 | tf_op jit(solution)/shard_map/slcd,ldf->slcf/dot_general | solution.py:164
  215.0 8.3 %fusion.32 = bf16[8,2,40,2048]{3,2,0,1:T(8,128)(2,1)S(1)} fusion(bf16[2,1408,2048]{2,1,0:T(8,128)(2,1)S(1)} %bitcast.161, f32[2,8,40,1408]{3,2,1,0:T(8,128)} %fusion.3, f32[2,8,40,1408]{3,2,1,0:T(8,128)} %fusion.5), kind=kOutput, calls=%fused_computation.44 | convolution fusion | flops 3697704960 | bytes 21364736 | tf_op jit(solution)/shard_map/slcf,lfd->slcd/dot_general | solution.py:341
  223.3 1.7 copy.36
  224.9 1.5 copy-done.4
  226.5 3.8 all-to-all-start.1
  230.3 24.1 %collective-permute-done.14.refs_5_ = bf16[4,3,64,768]{3,2,1,0:T(8,128)(2,1)} collective-permute-done((bf16[4,3,64,768]{3,2,1,0:T(8,128)(2,1)}, bf16[4,3,64,768]{3,2,1,0:T(8,128)(2,1)}, u32[]{:S(2)}, u32[]{:S(2)}) %collective-permute-start.14) | collective-permute-done | bytes 1179680 | tf_op jit(solution)/shard_map/ppermute | solution.py:235
  255.5 7.9 %shard_map.140 = (bf16[16,128,768]{2,1,0:T(8,128)(2,1)}, bf16[16,128,768]{2,1,0:T(8,128)(2,1)}, bf16[16,128,768]{2,1,0:T(8,128)(2,1)}) custom-call(s32[32]{0:T(128)} %pad_add_fusion.order_ref, bf16[4,3,64,768]{3,2,1,0:T(8,128)(2,1)} %pad_maximum_fusion.refs_0_, bf16[4,3,64,768]{3,2,1,0:T(8,128)(2,1)} %collective-permute-done.7.refs_1_, ...), custom_call_target="tpu_custom_call" | custom-call | flops 943718400 | bytes 18874368 | tf_op jit(solution)/shard_map/pallas_call | solution.py:184
  263.5 5.5 %fusion.104 = f32[512,768]{1,0:T(8,128)} fusion(bf16[512,2048]{1,0:T(8,128)(2,1)} %copy-done.16, bf16[2048,768]{1,0:T(8,128)(2,1)} %bitcast.164), kind=kOutput, calls=%fused_computation.191 | convolution fusion | flops 1610612736 | bytes 6815744 | tf_op jit(solution)/shard_map/dot_general | solution.py:160
  268.9 14.0 %fusion.15 = (bf16[8,2,40,1408]{3,2,0,1:T(8,128)(2,1)}, bf16[8,2,40,1408]{3,2,0,1:T(8,128)(2,1)}) fusion(f32[2,8,40,1408]{3,2,1,0:T(8,128)} %fusion.3, f32[2,8,40,1408]{3,2,1,0:T(8,128)} %fusion.5, bf16[2,1408,2048]{2,1,0:T(8,128)(2,1)} %param.24, bf16[8,2,40,2048]{3,2,1,0:T(8,128)(2,1)} %bitcast.148), kind=kOutput, calls=%fused_computation.26 | convolution fusion | flops 3702702080 | bytes 24969216 | tf_op jit(solution)/shard_map/slcd,lfd->slcf/dot_general | solution.py:345
  282.9 12.9 %fusion.29 = bf16[8,2,40,2048]{3,2,0,1:T(8,128)(2,1)S(1)} fusion(bf16[8,2,40,1408]{3,2,0,1:T(8,128)(2,1)} %get-tuple-element.18, bf16[8,2,40,1408]{3,2,0,1:T(8,128)(2,1)} %get-tuple-element.17, bf16[2,2048,1408]{2,1,0:T(8,128)(2,1)} %param.23, bf16[2,2048,1408]{2,1,0:T(8,128)(2,1)} %param.22), kind=kOutput, calls=%fused_computation.43 | convolution fusion | flops 7436632064 | bytes 29294592 | tf_op jit(solution)/shard_map/slcf,ldf->slcd/dot_general | solution.py:350
  295.8 1.9 copy.39
  297.7 4.6 %all-to-all-start.3 = ((bf16[8,80,2048]{2,1,0:T(8,128)(2,1)}), bf16[8,80,2048]{2,1,0:T(8,128)(2,1)}, u32[]{:S(2)}, u32[]{:S(2)}) async-start(bf16[8,80,2048]{2,1,0:T(8,128)(2,1)} %bitcast.37), calls=%async_computation.3 | async-start | bytes 5242880 | tf_op jit(solution)/shard_map/all_to_all | solution.py:238
  302.3 4.5 %fusion.102 = f32[512,768]{1,0:T(8,128)S(1)} fusion(bf16[512,2048]{1,0:T(8,128)(2,1)} %constant_dynamic-update-slice_fusion, bf16[2048,768]{1,0:T(8,128)(2,1)} %bitcast.166), kind=kOutput, calls=%fused_computation.189 | convolution fusion | flops 1610612736 | bytes 6815744 | tf_op jit(solution)/shard_map/dot_general | solution.py:160
  306.8 1.8 fusion.103
  308.6 1.8 fusion.55
  310.5 4.1 %add_multiply_fusion = f32[512,2048]{1,0:T(8,128)} fusion(f32[512,2048]{1,0:T(8,128)S(1)} %fusion.55, bf16[2048,768]{1,0:T(8,128)(2,1)S(1)} %bitcast.167, f32[512]{0:T(512)S(1)} %bitcast.152, f32[512,768]{1,0:T(8,128)S(1)} %fusion.102, f32[512,768]{1,0:T(8,128)S(1)} %copy-done.28, f32[512,768]{1,0:T(8,128)S(1)} %fusion.103), kind=kOutput, calls=%fused_computation.18 | convolution fusion | flops 1616642048 | bytes 16254976 | tf_op jit(solution)/shard_map/dot_general | solution.py:18
  314.6 1.9 multiply_reduce_fusion
  316.5 1.8 fusion.105
  318.4 2.0 select_reduce_fusion
  320.5 1.9 multiply_add_fusion
  322.4 2.0 copy-done.1
  325.2 2.6 collective-permute-start.23
  327.8 5.4 %all-to-all-done.3 = bf16[8,80,2048]{2,1,0:T(8,128)(2,1)} async-done(((bf16[8,80,2048]{2,1,0:T(8,128)(2,1)}), bf16[8,80,2048]{2,1,0:T(8,128)(2,1)}, u32[]{:S(2)}, u32[]{:S(2)}) %all-to-all-start.3) | async-done | bytes 2621472 | tf_op jit(solution)/shard_map/all_to_all | solution.py:238
  333.2 4.9 %convolution_add_fusion = f32[512,2048]{1,0:T(8,128)S(1)} fusion(f32[512,2048]{1,0:T(8,128)} %add_multiply_fusion, bf16[640,2048]{1,0:T(8,128)(2,1)} %bitcast.38, bf16[512,640]{1,0:T(8,128)(2,1)S(1)} %get-tuple-element.13), kind=kOutput, calls=%fused_computation.42 | convolution fusion | flops 1343225856 | bytes 11665408 | tf_op jit(solution)/shard_map/dot_general | solution.py:160
  338.9 2.4 collective-permute-start.18
  341.7 2.1 collective-permute-start.21
  343.9 33.2 %collective-permute-done.18 = bf16[128,2048]{1,0:T(8,128)(2,1)S(1)} collective-permute-done((bf16[128,2048]{1,0:T(8,128)(2,1)S(1)}, bf16[128,2048]{1,0:T(8,128)(2,1)S(1)}, u32[]{:S(2)}, u32[]{:S(2)}) %collective-permute-start.18) | collective-permute-done | bytes 524320 | tf_op jit(solution)/shard_map/ppermute | solution.py:235
  378.0 9.8 %collective-permute-done.21 = bf16[128,2048]{1,0:T(8,128)(2,1)S(1)} collective-permute-done((bf16[128,2048]{1,0:T(8,128)(2,1)S(1)}, bf16[128,2048]{1,0:T(8,128)(2,1)S(1)}, u32[]{:S(2)}, u32[]{:S(2)}) %collective-permute-start.21) | collective-permute-done | bytes 524320 | tf_op jit(solution)/shard_map/ppermute | solution.py:235
  387.9 1.6 fusion.52
  (158 shorter events, 36.8 us)
Async XLA Ops:
  0.6 29.0 %copy-start.3 = (bf16[128,2048]{1,0:T(8,128)(2,1)S(1)}, bf16[128,2048]{1,0:T(8,128)(2,1)}, u32[]{:S(2)}) copy-start(bf16[128,2048]{1,0:T(8,128)(2,1)} %param.13) | copy-start | bytes 1572868
  0.7 27.8 %collective-permute-start.2 = (bf16[128,2048]{1,0:T(8,128)(2,1)}, bf16[128,2048]{1,0:T(8,128)(2,1)S(1)}, u32[]{:S(2)}, u32[]{:S(2)}) collective-permute-start(bf16[128,2048]{1,0:T(8,128)(2,1)} %param.13), channel_id=1, source_target_pairs={{0,16},{1,17},{2,18},{3,19},{4,20},{5,21},{6,22},{7,23},{8,24},{9,... | collective-permute-start | bytes 1572872 | tf_op jit(solution)/shard_map/ppermute | solution.py:235
  10.6 23.6 %copy-start.21 = (f32[128]{0:T(128)}, f32[128]{0:T(128)S(1)}, u32[]{:S(2)}) copy-start(f32[128]{0:T(128)S(1)} %fusion.49) | copy-start | bytes 1540
  10.6 19.9 %collective-permute-start = (f32[128,13]{0,1:T(8,128)S(1)}, f32[128,13]{0,1:T(8,128)S(1)}, u32[]{:S(2)}, u32[]{:S(2)}) collective-permute-start(f32[128,13]{0,1:T(8,128)S(1)} %pad_maximum_fusion.11), channel_id=1, source_target_pairs={{0,16},{1,17},{2,18},{3,19},{4,20},{5,21},{6,22},{7,23},{8,24},{9,... | collective-permute-start | bytes 19976 | tf_op jit(solution)/shard_map/ppermute | solution.py:235
  29.6 4.6 %collective-permute-start.3 = (bf16[256,2048]{1,0:T(8,128)(2,1)S(1)}, bf16[256,2048]{1,0:T(8,128)(2,1)S(1)}, u32[]{:S(2)}, u32[]{:S(2)}) collective-permute-start(bf16[256,2048]{1,0:T(8,128)(2,1)S(1)} %pad_maximum_fusion.4), channel_id=1, source_target_pairs={{0,1},{1,0},{2,3},{3,2},{4,5},{5,4},{6,7},{7,6},{8,9},{9,8},{10,11... | collective-permute-start | bytes 3145736 | tf_op jit(solution)/shard_map/ppermute | solution.py:235
  30.5 1.8 collective-permute-start.1
  32.3 112.3 %copy-start.14 = (f32[512,13]{0,1:T(8,128)}, f32[512,13]{0,1:T(8,128)S(1)}, u32[]{:S(2)}) copy-start(f32[512,13]{0,1:T(8,128)S(1)} %pad_maximum_fusion.8) | copy-start | bytes 79876
  33.2 6.6 %copy-start.7 = (bf16[640,512]{1,0:T(8,128)(2,1)}, bf16[640,512]{1,0:T(8,128)(2,1)S(1)}, u32[]{:S(2)}) copy-start(bf16[640,512]{1,0:T(8,128)(2,1)S(1)} %convert_reduce_fusion) | copy-start | bytes 1966084
  39.8 5.5 %copy-start.11 = (bf16[2816,64]{0,1:T(8,128)(2,1)S(1)}, bf16[2816,64]{0,1:T(8,128)(2,1)}, u32[]{:S(2)}) copy-start(bf16[2816,64]{0,1:T(8,128)(2,1)} %param.21) | copy-start | bytes 1081348
  39.8 6.0 %copy-start.5 = (bf16[128,2048]{1,0:T(8,128)(2,1)S(1)}, bf16[128,2048]{1,0:T(8,128)(2,1)}, u32[]{:S(2)}) copy-start(bf16[128,2048]{1,0:T(8,128)(2,1)} %param.14) | copy-start | bytes 1572868
  39.8 84.6 %all-to-all-start = ((bf16[8,80,2048]{2,1,0:T(8,128)(2,1)}), bf16[8,80,2048]{2,1,0:T(8,128)(2,1)}, u32[]{:S(2)}, u32[]{:S(2)}) async-start(bf16[8,80,2048]{2,1,0:T(8,128)(2,1)} %bitcast.3), calls=%async_computation | async-start | bytes 5242880 | tf_op jit(solution)/shard_map/all_to_all | solution.py:238
  45.8 38.7 %collective-permute-start.10 = (bf16[128,2048]{1,0:T(8,128)(2,1)S(1)}, bf16[128,2048]{1,0:T(8,128)(2,1)}, u32[]{:S(2)}, u32[]{:S(2)}) collective-permute-start(bf16[128,2048]{1,0:T(8,128)(2,1)S(1)} %copy-done.5), channel_id=1, source_target_pairs={{0,16},{1,17},{2,18},{3,19},{4,20},{5,21},{6,22},{7,23},{8,24},{9,... | collective-permute-start | bytes 1572872 | tf_op jit(solution)/shard_map/ppermute | solution.py:235
  49.5 37.2 %copy-start.20 = (bf16[2048]{0:T(1024)(128)(2,1)S(1)}, bf16[2048]{0:T(1024)(128)(2,1)}, u32[]{:S(2)}) copy-start(bf16[2048]{0:T(1024)(128)(2,1)} %param.18) | copy-start | bytes 12292
  50.4 36.8 %collective-permute-start.4 = (bf16[2,3,64,768]{3,2,1,0:T(8,128)(2,1)}, bf16[2,3,64,768]{3,2,1,0:T(8,128)(2,1)}, u32[]{:S(2)}, u32[]{:S(2)}) collective-permute-start(bf16[2,3,64,768]{3,2,1,0:T(8,128)(2,1)} %get-tuple-element.26), channel_id=1, source_target_pairs={{0,1},{1,0},{2,3},{3,2},{4,5},{5,4},{6,7},{7,6},{8,9},{9,8},{10,11... | collective-permute-start | bytes 1769480 | tf_op jit(solution)/shard_map/ppermute | solution.py:235
  86.6 33.3 %collective-permute-start.19 = (bf16[256,2048]{1,0:T(8,128)(2,1)}, bf16[256,2048]{1,0:T(8,128)(2,1)S(1)}, u32[]{:S(2)}, u32[]{:S(2)}) collective-permute-start(bf16[256,2048]{1,0:T(8,128)(2,1)} %pad_maximum_fusion.5), channel_id=1, source_target_pairs={{0,1},{1,0},{2,3},{3,2},{4,5},{5,4},{6,7},{7,6},{8,9},{9,8},{10,11... | collective-permute-start | bytes 3145736 | tf_op jit(solution)/shard_map/ppermute | solution.py:235
  87.2 5.3 %copy-start.24 = (s32[16]{0:T(128)S(1)}, s32[16]{0:T(128)}, u32[]{:S(2)}) copy-start(s32[16]{0:T(128)} %constant.142.clone) | copy-start | bytes 196
  87.2 5.3 %copy-start.6 = (bf16[128,2048]{1,0:T(8,128)(2,1)S(1)}, bf16[128,2048]{1,0:T(8,128)(2,1)}, u32[]{:S(2)}) copy-start(bf16[128,2048]{1,0:T(8,128)(2,1)} %param.14) | copy-start | bytes 1572868
  89.0 32.4 %copy-start.8 = (bf16[640,512]{1,0:T(8,128)(2,1)S(1)}, bf16[640,512]{1,0:T(8,128)(2,1)}, u32[]{:S(2)}) copy-start(bf16[640,512]{1,0:T(8,128)(2,1)} %copy-done.7) | copy-start | bytes 1966084
  89.0 30.3 %collective-permute-start.11 = (bf16[3,128,768]{2,1,0:T(8,128)(2,1)S(1)}, bf16[3,128,768]{2,1,0:T(8,128)(2,1)}, u32[]{:S(2)}, u32[]{:S(2)}) collective-permute-start(bf16[3,128,768]{2,1,0:T(8,128)(2,1)S(1)} %get-tuple-element.8), channel_id=1, source_target_pairs={{0,16},{1,17},{2,18},{3,19},{4,20},{5,21},{6,22},{7,23},{8,24},{9,... | collective-permute-start | bytes 1769480 | tf_op jit(solution)/shard_map/ppermute | solution.py:235
  92.6 41.3 %collective-permute-start.5 = (bf16[3,128,768]{2,1,0:T(8,128)(2,1)S(1)}, bf16[3,128,768]{2,1,0:T(8,128)(2,1)}, u32[]{:S(2)}, u32[]{:S(2)}) collective-permute-start(bf16[3,128,768]{2,1,0:T(8,128)(2,1)S(1)} %bitcast.150), channel_id=1, source_target_pairs={{0,8},{1,9},{2,10},{3,11},{4,12},{5,13},{6,14},{7,15},{8,0},{9,1},... | collective-permute-start | bytes 1769480 | tf_op jit(solution)/shard_map/ppermute | solution.py:235
  119.3 19.9 %collective-permute-start.12 = (bf16[3,128,768]{2,1,0:T(8,128)(2,1)}, bf16[3,128,768]{2,1,0:T(8,128)(2,1)}, u32[]{:S(2)}, u32[]{:S(2)}) collective-permute-start(bf16[3,128,768]{2,1,0:T(8,128)(2,1)} %collective-permute-done.11), channel_id=1, source_target_pairs={{0,8},{1,9},{2,10},{3,11},{4,12},{5,13},{6,14},{7,15},{8,0},{9,1},... | collective-permute-start | bytes 1769480 | tf_op jit(solution)/shard_map/ppermute | solution.py:235
  124.4 100.5 %all-to-all-start.2 = ((bf16[8,80,2048]{2,1,0:T(8,128)(2,1)}), bf16[8,80,2048]{2,1,0:T(8,128)(2,1)S(1)}, u32[]{:S(2)}, u32[]{:S(2)}) async-start(bf16[8,80,2048]{2,1,0:T(8,128)(2,1)} %bitcast.149), calls=%async_computation.2 | async-start | bytes 5242880 | tf_op jit(solution)/shard_map/all_to_all | solution.py:238
  133.9 10.7 %copy-start.22 = (f32[128]{0:T(128)S(1)}, f32[128]{0:T(128)}, u32[]{:S(2)}) copy-start(f32[128]{0:T(128)} %copy-done.21) | copy-start | bytes 1540
  135.0 43.4 %collective-permute-start.6 = (bf16[2,3,64,768]{3,2,1,0:T(8,128)(2,1)S(1)}, bf16[2,3,64,768]{3,2,1,0:T(8,128)(2,1)S(1)}, u32[]{:S(2)}, u32[]{:S(2)}) collective-permute-start(bf16[2,3,64,768]{3,2,1,0:T(8,128)(2,1)S(1)} %get-tuple-element.24), channel_id=1, source_target_pairs={{0,2},{1,3},{2,0},{3,1},{4,6},{5,7},{6,4},{7,5},{8,10},{9,11},{10,... | collective-permute-start | bytes 1769480 | tf_op jit(solution)/shard_map/ppermute | solution.py:235
  137.7 43.3 %collective-permute-start.8 = (bf16[2,3,64,768]{3,2,1,0:T(8,128)(2,1)S(1)}, bf16[2,3,64,768]{3,2,1,0:T(8,128)(2,1)S(1)}, u32[]{:S(2)}, u32[]{:S(2)}) collective-permute-start(bf16[2,3,64,768]{3,2,1,0:T(8,128)(2,1)S(1)} %get-tuple-element.23), channel_id=1, source_target_pairs={{0,4},{1,5},{2,6},{3,7},{4,0},{5,1},{6,2},{7,3},{8,12},{9,13},{10,... | collective-permute-start | bytes 1769480 | tf_op jit(solution)/shard_map/ppermute | solution.py:235
  140.5 53.2 %collective-permute-start.15 = (bf16[2,3,64,768]{3,2,1,0:T(8,128)(2,1)S(1)}, bf16[2,3,64,768]{3,2,1,0:T(8,128)(2,1)S(1)}, u32[]{:S(2)}, u32[]{:S(2)}) collective-permute-start(bf16[2,3,64,768]{3,2,1,0:T(8,128)(2,1)S(1)} %get-tuple-element.19), channel_id=1, source_target_pairs={{0,4},{1,5},{2,6},{3,7},{4,0},{5,1},{6,2},{7,3},{8,12},{9,13},{10,... | collective-permute-start | bytes 1769480 | tf_op jit(solution)/shard_map/ppermute | solution.py:235
  141.1 50.0 %collective-permute-start.13 = (bf16[2,3,64,768]{3,2,1,0:T(8,128)(2,1)S(1)}, bf16[2,3,64,768]{3,2,1,0:T(8,128)(2,1)S(1)}, u32[]{:S(2)}, u32[]{:S(2)}) collective-permute-start(bf16[2,3,64,768]{3,2,1,0:T(8,128)(2,1)S(1)} %get-tuple-element.20), channel_id=1, source_target_pairs={{0,2},{1,3},{2,0},{3,1},{4,6},{5,7},{6,4},{7,5},{8,10},{9,11},{10,... | collective-permute-start | bytes 1769480 | tf_op jit(solution)/shard_map/ppermute | solution.py:235
  179.5 50.7 %collective-permute-start.7 = (bf16[4,3,64,768]{3,2,1,0:T(8,128)(2,1)}, bf16[4,3,64,768]{3,2,1,0:T(8,128)(2,1)}, u32[]{:S(2)}, u32[]{:S(2)}) collective-permute-start(bf16[4,3,64,768]{3,2,1,0:T(8,128)(2,1)} %pad_maximum_fusion.refs_0_), channel_id=1, source_target_pairs={{0,4},{1,5},{2,6},{3,7},{4,0},{5,1},{6,2},{7,3},{8,12},{9,13},{10,... | collective-permute-start | bytes 3538952 | tf_op jit(solution)/shard_map/ppermute | solution.py:235
  182.2 48.1 %collective-permute-start.9 = (bf16[4,3,64,768]{3,2,1,0:T(8,128)(2,1)}, bf16[4,3,64,768]{3,2,1,0:T(8,128)(2,1)}, u32[]{:S(2)}, u32[]{:S(2)}) collective-permute-start(bf16[4,3,64,768]{3,2,1,0:T(8,128)(2,1)} %pad_maximum_fusion.1.refs_2_), channel_id=1, source_target_pairs={{0,2},{1,3},{2,0},{3,1},{4,6},{5,7},{6,4},{7,5},{8,10},{9,11},{10,... | collective-permute-start | bytes 3538952 | tf_op jit(solution)/shard_map/ppermute | solution.py:235
  192.2 62.2 %collective-permute-start.14 = (bf16[4,3,64,768]{3,2,1,0:T(8,128)(2,1)}, bf16[4,3,64,768]{3,2,1,0:T(8,128)(2,1)}, u32[]{:S(2)}, u32[]{:S(2)}) collective-permute-start(bf16[4,3,64,768]{3,2,1,0:T(8,128)(2,1)} %pad_maximum_fusion.2.refs_4_), channel_id=1, source_target_pairs={{0,4},{1,5},{2,6},{3,7},{4,0},{5,1},{6,2},{7,3},{8,12},{9,13},{10,... | collective-permute-start | bytes 3538952 | tf_op jit(solution)/shard_map/ppermute | solution.py:235
  193.7 13.3 %slice-start.4 = ((s8[11534336]{0:T(1024)(128)(4,1)}), s8[4194304]{0:T(1024)(128)(4,1)S(1)}, s32[]{:S(2)}) async-start(s8[11534336]{0:T(1024)(128)(4,1)} %bitcast.162), calls=%async_computation.8 | async-start | bytes 8388608
  194.8 60.7 %collective-permute-start.16 = (bf16[4,3,64,768]{3,2,1,0:T(8,128)(2,1)}, bf16[4,3,64,768]{3,2,1,0:T(8,128)(2,1)}, u32[]{:S(2)}, u32[]{:S(2)}) collective-permute-start(bf16[4,3,64,768]{3,2,1,0:T(8,128)(2,1)} %pad_maximum_fusion.3.refs_6_), channel_id=1, source_target_pairs={{0,2},{1,3},{2,0},{3,1},{4,6},{5,7},{6,4},{7,5},{8,10},{9,11},{10,... | collective-permute-start | bytes 3538952 | tf_op jit(solution)/shard_map/ppermute | solution.py:235
  195.7 11.2 %slice-start.5 = ((s8[11534336]{0:T(1024)(128)(4,1)}), s8[4194304]{0:T(1024)(128)(4,1)S(1)}, s32[]{:S(2)}) async-start(s8[11534336]{0:T(1024)(128)(4,1)} %bitcast.162), calls=%async_computation.9 | async-start | bytes 8388608
  195.7 11.2 %slice-start.6 = ((s8[11534336]{0:T(1024)(128)(4,1)}), s8[3145728]{0:T(1024)(128)(4,1)S(1)}, s32[]{:S(2)}) async-start(s8[11534336]{0:T(1024)(128)(4,1)} %bitcast.162), calls=%async_computation.10 | async-start | bytes 6291456
  195.7 19.3 %slice-start.1 = ((s8[11534336]{0:T(1024)(128)(4,1)}), s8[4194304]{0:T(1024)(128)(4,1)S(1)}, s32[]{:S(2)}) async-start(s8[11534336]{0:T(1024)(128)(4,1)} %bitcast.160), calls=%async_computation.5 | async-start | bytes 8388608
  195.7 19.3 %slice-start.2 = ((s8[11534336]{0:T(1024)(128)(4,1)}), s8[4194304]{0:T(1024)(128)(4,1)S(1)}, s32[]{:S(2)}) async-start(s8[11534336]{0:T(1024)(128)(4,1)} %bitcast.160), calls=%async_computation.6 | async-start | bytes 8388608
  207.0 8.0 %slice-start.3 = ((s8[11534336]{0:T(1024)(128)(4,1)}), s8[3145728]{0:T(1024)(128)(4,1)S(1)}, s32[]{:S(2)}) async-start(s8[11534336]{0:T(1024)(128)(4,1)} %bitcast.160), calls=%async_computation.7 | async-start | bytes 6291456
  226.5 71.2 %all-to-all-start.1 = ((bf16[8,80,2048]{2,1,0:T(8,128)(2,1)}), bf16[8,80,2048]{2,1,0:T(8,128)(2,1)S(1)}, u32[]{:S(2)}, u32[]{:S(2)}) async-start(bf16[8,80,2048]{2,1,0:T(8,128)(2,1)} %bitcast.14), calls=%async_computation.1 | async-start | bytes 5242880 | tf_op jit(solution)/shard_map/all_to_all | solution.py:238
  297.7 35.5 %all-to-all-start.3 = ((bf16[8,80,2048]{2,1,0:T(8,128)(2,1)}), bf16[8,80,2048]{2,1,0:T(8,128)(2,1)}, u32[]{:S(2)}, u32[]{:S(2)}) async-start(bf16[8,80,2048]{2,1,0:T(8,128)(2,1)} %bitcast.37), calls=%async_computation.3 | async-start | bytes 5242880 | tf_op jit(solution)/shard_map/all_to_all | solution.py:238
  320.4 4.7 %collective-permute-start.22 = (f32[256,5]{0,1:T(8,128)S(1)}, f32[256,5]{0,1:T(8,128)S(1)}, u32[]{:S(2)}, u32[]{:S(2)}) collective-permute-start(f32[256,5]{0,1:T(8,128)S(1)} %pad_maximum_fusion.10), channel_id=1, source_target_pairs={{0,1},{1,0},{2,3},{3,2},{4,5},{5,4},{6,7},{7,6},{8,9},{9,8},{10,11... | collective-permute-start | bytes 15368 | tf_op jit(solution)/shard_map/ppermute | solution.py:235
  324.6 13.8 %collective-permute-start.17 = (bf16[256,2048]{1,0:T(8,128)(2,1)S(1)}, bf16[256,2048]{1,0:T(8,128)(2,1)S(1)}, u32[]{:S(2)}, u32[]{:S(2)}) collective-permute-start(bf16[256,2048]{1,0:T(8,128)(2,1)S(1)} %slice.157), channel_id=1, source_target_pairs={{0,1},{1,0},{2,3},{3,2},{4,5},{5,4},{6,7},{7,6},{8,9},{9,8},{10,11... | collective-permute-start | bytes 3145736 | tf_op jit(solution)/shard_map/ppermute | solution.py:235
  325.2 13.2 %collective-permute-start.23 = (f32[128,5]{0,1:T(8,128)S(1)}, f32[128,5]{0,1:T(8,128)S(1)}, u32[]{:S(2)}, u32[]{:S(2)}) collective-permute-start(f32[128,5]{0,1:T(8,128)S(1)} %slice.110), channel_id=1, source_target_pairs={{0,16},{1,17},{2,18},{3,19},{4,20},{5,21},{6,22},{7,23},{8,24},{9,... | collective-permute-start | bytes 7688 | tf_op jit(solution)/shard_map/ppermute | solution.py:235
  333.2 5.2 %copy-start.2 = (f32[512,2048]{1,0:T(8,128)S(1)}, f32[512,2048]{1,0:T(8,128)}, u32[]{:S(2)}) copy-start(f32[512,2048]{1,0:T(8,128)} %copy-done.1) | copy-start | bytes 12582916
  338.3 3.0 collective-permute-start.20
  338.9 38.2 %collective-permute-start.18 = (bf16[128,2048]{1,0:T(8,128)(2,1)S(1)}, bf16[128,2048]{1,0:T(8,128)(2,1)S(1)}, u32[]{:S(2)}, u32[]{:S(2)}) collective-permute-start(bf16[128,2048]{1,0:T(8,128)(2,1)S(1)} %slice.159), channel_id=1, source_target_pairs={{0,16},{1,17},{2,18},{3,19},{4,20},{5,21},{6,22},{7,23},{8,24},{9,... | collective-permute-start | bytes 1572872 | tf_op jit(solution)/shard_map/ppermute | solution.py:235
  341.6 46.2 %copy-start.13 = (f32[128,60]{0,1:T(8,128)S(1)}, f32[128,60]{0,1:T(8,128)}, u32[]{:S(2)}) copy-start(f32[128,60]{0,1:T(8,128)} %copy-done.12) | copy-start | bytes 92164
  341.6 46.2 %copy-start.18 = (f32[2048]{0:T(1024)S(1)}, f32[2048]{0:T(1024)}, u32[]{:S(2)}) copy-start(f32[2048]{0:T(1024)} %convert_element_type.118) | copy-start | bytes 24580
  341.7 46.1 %collective-permute-start.21 = (bf16[128,2048]{1,0:T(8,128)(2,1)S(1)}, bf16[128,2048]{1,0:T(8,128)(2,1)S(1)}, u32[]{:S(2)}, u32[]{:S(2)}) collective-permute-start(bf16[128,2048]{1,0:T(8,128)(2,1)S(1)} %slice.158), channel_id=1, source_target_pairs={{0,16},{1,17},{2,18},{3,19},{4,20},{5,21},{6,22},{7,23},{8,24},{9,... | collective-permute-start | bytes 1572872 | tf_op jit(solution)/shard_map/ppermute | solution.py:235
  (16 other events, 56.1 us)
where the time goes:
time: 397 us; the launch traced here: 390 us
  waiting for transfers between devices  193 us (49%)
  matrix products  94.6 us (24%)
  starting transfers between devices  56 us (14%)
  other arithmetic  20.7 us (5%)
  local copies, waits for them, and re-layouts  16.2 us (4%)
  Pallas kernels  7.95 us (2%)
    ppermute x24, waiting for transfers between devices, across(): return lax.ppermute(value, 'dp', pairs)  187 us
    ppermute x24, starting transfers between devices, across(): return lax.ppermute(value, 'dp', pairs)  33.6 us
    dot_general x10, matrix products, dot32(): return jnp.dot(left, right, preferred_element_type=jnp.float32)  29 us
    all_to_all x4, starting transfers between devices, exchange(): lax.all_to_all(value, 'dp', split_axis=0, concat_axis=0, tiled=True, axis...  22.4 us
    dot_general x1, matrix products, paired_shards(): jnp.einsum('slcd,lfd->slcf', got_cot, ex_down, preferred_element_type=jnp...  14 us
    dot_general x1, matrix products, paired_shards(): jnp.einsum('slcf,ldf->slcd', grad_both, weight_both, preferred_element_ty...  12.9 us
    dot_general x1, matrix products, expert_hidden(): jnp.einsum('slcd,ldf->slcf', rows_in, w_up, preferred_element_type=jnp.fl...  11.2 us
    dot_general x4, matrix products, contract_last(): lax.dot_general(left, right, (((1,), (1,)), ((), ())), preferred_element_...  9.68 us
  transfers between devices with their start and end apart: 28, of which 11 were waited for; matrix products, arithmetic and copies ran while one was open for 31% of the time, Pallas kernels for 2%

commit v1 on v0

--- a/solution.py
+++ b/solution.py
@@ -219,8 +219,11 @@
     half_size = dp_size // 2
     lanes = half_size // 2
     lane_bits = lanes.bit_length() - 1
-    rows_slot = -(-4 * CAP // 8) * 8
-    rows_all = lanes * local_slots * rows_slot
+    rows_main = 4 * CAP // 8 * 8
+    rows_last = 4 * CAP - rows_main
+    rows_shared = -(-rows_last * local_slots // 8) * 8
+    rows_lane = local_slots * rows_main + rows_shared
+    rows_all = lanes * rows_lane
     me = lax.axis_index("dp")
     half = me // half_size
     lane = (me % half_size) // 2
@@ -273,8 +276,14 @@
     scale_all = meta_all[:, 3 * top_count :]
     holder = slot_all // local_slots
     block = jnp.arange(tok_all, dtype=jnp.int32)[:, None] // tok_dev
-    row_at = ((holder % half_size) // 2) * local_slots + slot_all % local_slots
-    row_at = row_at * rows_slot + block * CAP + rank_all
+    inside = block * CAP + rank_all
+    local = slot_all % local_slots
+    inside = jnp.where(
+        inside < rows_main,
+        local * rows_main + inside,
+        local_slots * rows_main + local * rows_last + inside - rows_main,
+    )
+    row_at = ((holder % half_size) // 2) * rows_lane + inside
     row_at = jnp.where((holder // half_size == half) & (holder % 2 == core), row_at, -1)
     row_ids = jnp.arange(rows_all, dtype=jnp.int32)
     pick_rows = jnp.sum(
@@ -285,11 +294,22 @@
 
     def dispatch(table):
         rows = dot32(pick_rows, table).astype(jnp.bfloat16)
-        got = exchange(rows.reshape(lanes, local_slots * rows_slot, width))
-        return got.reshape(lanes, local_slots, rows_slot, width)
-
-    def give_back(rows):
-        sent = rows.reshape(lanes, local_slots * rows_slot, width)
+        got = exchange(rows.reshape(lanes, rows_lane, width))
+        main = got[:, : local_slots * rows_main].reshape(lanes, local_slots, rows_main, width)
+        last = jnp.broadcast_to(
+            got[:, None, local_slots * rows_main :], (lanes, local_slots, rows_shared, width)
+        )
+        return jnp.concatenate([main, last], axis=2)
+
+    def pack(rows):
+        main = rows[:, :, :rows_main].reshape(lanes, local_slots * rows_main, width)
+        owner = jnp.arange(rows_shared, dtype=jnp.int32)[None, :, None] // max(rows_last, 1)
+        last = rows[:, 0, rows_main:]
+        for local in range(1, local_slots):
+            last = jnp.where(owner == local, rows[:, local, rows_main:], last)
+        return jnp.concatenate([main, last], axis=1)
+
+    def give_back(sent):
         return exchange(sent).reshape(rows_all, width)
 
     got_in = dispatch(tokens_all)
@@ -337,20 +357,24 @@
 
     pre_gate, pre_up = expert_hidden(got_in, ex_gate, ex_up)
     active, derivative = silu_pair(pre_gate)
-    hidden = (active * pre_up).astype(jnp.bfloat16)
+    hidden, active, slope = lax.optimization_barrier(
+        ((active * pre_up).astype(jnp.bfloat16), active, pre_up * derivative)
+    )
     result = jnp.einsum(
         "slcf,lfd->slcd", hidden, ex_down, preferred_element_type=jnp.float32
     ).astype(jnp.bfloat16)
-    routed_out = give_back(result)
+    sent_out = after(pack(result), place)
+    routed_out = give_back(sent_out)
+    got_cot = after(got_cot, sent_out)
     grad_hidden = jnp.einsum("slcd,lfd->slcf", got_cot, ex_down, preferred_element_type=jnp.float32)
-    grad_gate = (grad_hidden * pre_up * derivative).astype(jnp.bfloat16)
+    grad_gate = (grad_hidden * slope).astype(jnp.bfloat16)
     grad_up = (grad_hidden * active).astype(jnp.bfloat16)
     grad_both = jnp.concatenate([grad_gate, grad_up], axis=3)
     weight_both = jnp.concatenate([ex_gate, ex_up], axis=2)
     backward = jnp.einsum(
         "slcf,ldf->slcd", grad_both, weight_both, preferred_element_type=jnp.float32
     ).astype(jnp.bfloat16)
-    routed_back = give_back(backward)
+    routed_back = give_back(pack(backward))
 
     own_stacks, own_lows, sources = spread(own_rows)
     far_stacks, far_lows, _ = spread(far_rows)
@@ -370,7 +394,7 @@
     sh_hidden = (sh_active * sh_pre_up).astype(jnp.bfloat16)
     sh_out = contract_last(sh_hidden, full_down)
     mixed_part = dot32(place, routed_out) + scale_all * sh_out
-    sh_grad_hidden = dot32(grads_all, full_down)
+    sh_grad_hidden = dot32(after(grads_all, mixed_part), full_down)
     sh_grad_gate = (sh_grad_hidden * sh_pre_up * sh_derivative).astype(jnp.bfloat16)
     sh_grad_up = (sh_grad_hidden * sh_active).astype(jnp.bfloat16)
     sh_back = contract_last(sh_grad_gate, full_gate) + contract_last(sh_grad_up, full_up)

time: 397 us -> 369 us (0.929)
  starting transfers between devices: 56 us -> 41.3 us
  waiting for transfers between devices: 193 us -> 187 us
  matrix products: 94.6 us -> 90.1 us
    ppermute x24, starting transfers between devices: 33.6 us -> 20.5 us  [across(): return lax.ppermute(value, 'dp', pairs)]
    ppermute x24, waiting for transfers between devices: 187 us -> 178 us  [across(): return lax.ppermute(value, 'dp', pairs)]
    concatenate x0 -> x3, other arithmetic: none -> 4.96 us  [the longest x2 3.15 us: pack(): return jnp.concatenate([main, last], axis=1)]
    concatenate x4, other arithmetic: 4.57 us -> 0.42 us  [spread(): held = jnp.concatenate([held, received], axis=0)]
    all_to_all x4, waiting for transfers between devices: 5.41 us -> 9.46 us  [exchange(): lax.all_to_all(value, 'dp', split_axis=0, concat_axis=0, tiled=True, axis...]
    unnamed x75 -> x83, local copies, waits for them, and re-layouts: 8.63 us -> 7.48 us
  transfers between devices with their start and end apart: 28 -> 28, of which waited for: 11 -> 12; matrix products, arithmetic and copies ran while one was open for 31% -> 33% of each run, Pallas kernels for 2% -> 2%
where the time goes in v1:
time: 369 us; the launch traced here: 364 us
  waiting for transfers between devices  187 us (51%)
  matrix products  90.1 us (24%)
  starting transfers between devices  41.3 us (11%)
  other arithmetic  18.8 us (5%)
  local copies, waits for them, and re-layouts  16.2 us (4%)
  Pallas kernels  8.07 us (2%)
    ppermute x24, waiting for transfers between devices, across(): return lax.ppermute(value, 'dp', pairs)  178 us
    dot_general x10, matrix products, dot32(): return jnp.dot(left, right, preferred_element_type=jnp.float32)  25.6 us
    all_to_all x4, starting transfers between devices, exchange(): lax.all_to_all(value, 'dp', split_axis=0, concat_axis=0, tiled=True, axis...  20.8 us
    ppermute x24, starting transfers between devices, across(): return lax.ppermute(value, 'dp', pairs)  20.5 us
    dot_general x1, matrix products, paired_shards(): jnp.einsum('slcd,lfd->slcf', got_cot, ex_down, preferred_element_type=jnp...  13.3 us
    dot_general x1, matrix products, paired_shards(): jnp.einsum('slcf,ldf->slcd', grad_both, weight_both, preferred_element_ty...  12.9 us
    dot_general x1, matrix products, expert_hidden(): jnp.einsum('slcd,ldf->slcf', rows_in, w_up, preferred_element_type=jnp.fl...  11.7 us
    dot_general x4, matrix products, contract_last(): lax.dot_general(left, right, (((1,), (1,)), ((), ())), preferred_element_...  11.3 us
  transfers between devices with their start and end apart: 28, of which 12 were waited for; matrix products, arithmetic and copies ran while one was open for 33% of the time, Pallas kernels for 2%

profile of v1, /device:TPU:0, one launch (start us, length us, event | category | flops | bytes accessed | tf_op | source)
XLA Modules:
  0.0 363.6 jit_solution(7083920714895045880)
XLA Ops:
  0.7 4.1 %collective-permute-start.2 = (bf16[128,2048]{1,0:T(8,128)(2,1)}, bf16[128,2048]{1,0:T(8,128)(2,1)}, u32[]{:S(2)}, u32[]{:S(2)}) collective-permute-start(bf16[128,2048]{1,0:T(8,128)(2,1)} %param.13), channel_id=1, source_target_pairs={{0,16},{1,17},{2,18},{3,19},{4,20},{5,21},{6,22},{7,23},{8,24},{9,... | collective-permute-start | bytes 1572872 | tf_op jit(solution)/shard_map/ppermute | solution.py:238
  8.4 1.4 fusion.94
  10.8 1.4 stack.28
  15.7 12.8 %collective-permute-done = f32[128,13]{0,1:T(8,128)S(1)} collective-permute-done((f32[128,13]{0,1:T(8,128)S(1)}, f32[128,13]{0,1:T(8,128)S(1)}, u32[]{:S(2)}, u32[]{:S(2)}) %collective-permute-start) | collective-permute-done | bytes 6688 | tf_op jit(solution)/shard_map/ppermute | solution.py:238
  31.2 2.1 constant_dynamic-update-slice_fusion.1
  33.3 1.7 maximum_select_fusion
  36.0 4.1 %collective-permute-start.5 = (bf16[3,128,768]{2,1,0:T(8,128)(2,1)S(1)}, bf16[3,128,768]{2,1,0:T(8,128)(2,1)}, u32[]{:S(2)}, u32[]{:S(2)}) collective-permute-start(bf16[3,128,768]{2,1,0:T(8,128)(2,1)S(1)} %bitcast.166), channel_id=1, source_target_pairs={{0,8},{1,9},{2,10},{3,11},{4,12},{5,13},{6,14},{7,15},{8,0},{9,1},... | collective-permute-start | bytes 1769480 | tf_op jit(solution)/shard_map/ppermute | solution.py:238
  40.0 16.6 %collective-permute-done.10 = bf16[128,2048]{1,0:T(8,128)(2,1)S(1)} collective-permute-done((bf16[128,2048]{1,0:T(8,128)(2,1)S(1)}, bf16[128,2048]{1,0:T(8,128)(2,1)S(1)}, u32[]{:S(2)}, u32[]{:S(2)}) %collective-permute-start.10) | collective-permute-done | bytes 524320 | tf_op jit(solution)/shard_map/ppermute | solution.py:238
  56.8 2.8 convolution_convert_fusion.1
  59.6 5.4 %all-to-all-start = ((bf16[8,72,2048]{2,1,0:T(8,128)(2,1)}), bf16[8,72,2048]{2,1,0:T(8,128)(2,1)S(1)}, u32[]{:S(2)}, u32[]{:S(2)}) async-start(bf16[8,72,2048]{2,1,0:T(8,128)(2,1)} %bitcast.164), calls=%async_computation | async-start | bytes 4718592 | tf_op jit(solution)/shard_map/all_to_all | solution.py:241
  65.0 19.4 %collective-permute-done.11 = bf16[3,128,768]{2,1,0:T(8,128)(2,1)} collective-permute-done((bf16[3,128,768]{2,1,0:T(8,128)(2,1)}, bf16[3,128,768]{2,1,0:T(8,128)(2,1)}, u32[]{:S(2)}, u32[]{:S(2)}) %collective-permute-start.11) | collective-permute-done | bytes 589856 | tf_op jit(solution)/shard_map/ppermute | solution.py:238
  86.7 1.6 collective-permute-start.6
  88.3 1.5 collective-permute-start.8
  89.8 27.9 %collective-permute-done.12 = bf16[3,128,768]{2,1,0:T(8,128)(2,1)S(1)} collective-permute-done((bf16[3,128,768]{2,1,0:T(8,128)(2,1)}, bf16[3,128,768]{2,1,0:T(8,128)(2,1)S(1)}, u32[]{:S(2)}, u32[]{:S(2)}) %collective-permute-start.12) | collective-permute-done | bytes 589856 | tf_op jit(solution)/shard_map/ppermute | solution.py:238
  118.9 1.5 collective-permute-start.13
  121.5 1.5 collective-permute-start.15
  124.7 10.4 %collective-permute-done.13 = bf16[2,3,64,768]{3,2,1,0:T(8,128)(2,1)S(1)} collective-permute-done((bf16[2,3,64,768]{3,2,1,0:T(8,128)(2,1)S(1)}, bf16[2,3,64,768]{3,2,1,0:T(8,128)(2,1)S(1)}, u32[]{:S(2)}, u32[]{:S(2)}) %collective-permute-start.13) | collective-permute-done | bytes 589856 | tf_op jit(solution)/shard_map/ppermute | solution.py:238
  135.3 1.5 collective-permute-start.14
  139.6 2.8 convolution_convert_fusion
  142.4 20.7 %collective-permute-done.7.refs_1_ = bf16[4,3,64,768]{3,2,1,0:T(8,128)(2,1)S(1)} collective-permute-done((bf16[4,3,64,768]{3,2,1,0:T(8,128)(2,1)S(1)}, bf16[4,3,64,768]{3,2,1,0:T(8,128)(2,1)S(1)}, u32[]{:S(2)}, u32[]{:S(2)}) %collective-permute-start.7) | collective-permute-done | bytes 1179680 | tf_op jit(solution)/shard_map/ppermute | solution.py:238
  163.0 22.6 %collective-permute-done.14.refs_5_ = bf16[4,3,64,768]{3,2,1,0:T(8,128)(2,1)S(1)} collective-permute-done((bf16[4,3,64,768]{3,2,1,0:T(8,128)(2,1)S(1)}, bf16[4,3,64,768]{3,2,1,0:T(8,128)(2,1)S(1)}, u32[]{:S(2)}, u32[]{:S(2)}) %collective-permute-start.14) | collective-permute-done | bytes 1179680 | tf_op jit(solution)/shard_map/ppermute | solution.py:238
  186.7 8.1 %shard_map.140 = (bf16[16,128,768]{2,1,0:T(8,128)(2,1)}, bf16[16,128,768]{2,1,0:T(8,128)(2,1)}, bf16[16,128,768]{2,1,0:T(8,128)(2,1)}) custom-call(s32[32]{0:T(128)} %pad_add_fusion.order_ref, bf16[4,3,64,768]{3,2,1,0:T(8,128)(2,1)} %copy-done.2, bf16[4,3,64,768]{3,2,1,0:T(8,128)(2,1)} %copy-done.12, bf16[4,3,64,768]{3,2,1,0:T(8,128)(2,1)} %copy-done.3, ...), custom_call_target="tpu_custom_call" | custom-call | flops 943718400 | bytes 18874368 | tf_op jit(solution)/shard_map/pallas_call | solution.py:184
  194.8 5.6 %fusion.96 = f32[512,768]{1,0:T(8,128)} fusion(bf16[512,2048]{1,0:T(8,128)(2,1)} %copy-done.22, bf16[2048,768]{1,0:T(8,128)(2,1)} %bitcast.181), kind=kOutput, calls=%fused_computation.199 | convolution fusion | flops 1610612736 | bytes 6815744 | tf_op jit(solution)/shard_map/dot_general | solution.py:160
  200.4 3.0 fusion.97
  203.4 4.9 %all-to-all-start.2 = ((bf16[8,72,2048]{2,1,0:T(8,128)(2,1)}), bf16[8,72,2048]{2,1,0:T(8,128)(2,1)}, u32[]{:S(2)}, u32[]{:S(2)}) async-start(bf16[8,72,2048]{2,1,0:T(8,128)(2,1)} %bitcast.165), calls=%async_computation.2 | async-start | bytes 4718592 | tf_op jit(solution)/shard_map/all_to_all | solution.py:241
  208.5 9.1 %fusion.5 = f32[2,8,40,1408]{3,2,1,0:T(8,128)} fusion(bf16[2,2048,1408]{2,1,0:T(8,128)(2,1)} %param.22, bf16[8,2,8,2048]{3,2,0,1:T(8,128)(2,1)S(1)} %broadcast_in_dim.44, bf16[8,2,32,2048]{3,2,1,0:T(8,128)(2,1)S(1)} %bitcast.167), kind=kOutput, calls=%fused_computation.6 | convolution fusion | flops 3696230400 | bytes 17760256 | tf_op jit(solution)/shard_map/slcd,ldf->slcf/dot_general | solution.py:164
  217.6 11.7 %bitcast_multiply_fusion.2 = (f32[8,2,40,1408]{3,2,0,1:T(8,128)}, bf16[8,2,40,1408]{3,2,0,1:T(8,128)(2,1)S(1)}, f32[8,2,40,1408]{3,2,0,1:T(8,128)}) fusion(f32[2,8,40,1408]{3,2,1,0:T(8,128)} %fusion.5, bf16[2,2048,1408]{2,1,0:T(8,128)(2,1)} %param.23, bf16[8,2,8,2048]{3,2,0,1:T(8,128)(2,1)S(1)} %broadcast_in_dim.44, bf16[8,2,32,2048]{3,2,1,0:T(8,128)(2,1)S(1)} %bitcast.168), kind=kOutput, calls=%fused_computation.27 | convolution fusion | flops 3706142720 | bytes 26771456 | tf_op jit(solution)/shard_map/slcd,ldf->slcf/dot_general | solution.py:165
  229.4 4.6 %fusion.31 = bf16[8,2,40,2048]{3,2,0,1:T(8,128)(2,1)S(1)} fusion(bf16[8,2,40,1408]{3,2,0,1:T(8,128)(2,1)S(1)} %get-tuple-element.13, bf16[2,1408,2048]{2,1,0:T(8,128)(2,1)S(1)} %bitcast.180), kind=kOutput, calls=%fused_computation.44 | convolution fusion | flops 3692298240 | bytes 15958016 | tf_op jit(solution)/shard_map/slcf,lfd->slcd/dot_general | solution.py:363
  234.4 1.6 pad_maximum_fusion.2
  236.0 5.3 %all-to-all-start.1 = ((bf16[8,72,2048]{2,1,0:T(8,128)(2,1)}), bf16[8,72,2048]{2,1,0:T(8,128)(2,1)S(1)}, u32[]{:S(2)}, u32[]{:S(2)}) async-start(bf16[8,72,2048]{2,1,0:T(8,128)(2,1)} %pad_maximum_fusion.2), calls=%async_computation.1 | async-start | bytes 4718592 | tf_op jit(solution)/shard_map/all_to_all | solution.py:241
  242.3 1.8 slice.148
  244.2 1.8 pad_maximum_fusion.1
  246.0 13.3 %fusion.14 = (bf16[8,2,40,1408]{3,2,0,1:T(8,128)(2,1)}, bf16[8,2,40,1408]{3,2,0,1:T(8,128)(2,1)}) fusion(f32[8,2,40,1408]{3,2,0,1:T(8,128)} %get-tuple-element.21, f32[8,2,40,1408]{3,2,0,1:T(8,128)} %get-tuple-element.22, bf16[2,1408,2048]{2,1,0:T(8,128)(2,1)} %param.24, bf16[8,2,40,2048]{3,2,1,0:T(8,128)(2,1)} %pad_maximum_fusion.1), kind=kOutput, calls=%fused_computation.25 | convolution fusion | flops 3694592000 | bytes 24969216 | tf_op jit(solution)/shard_map/slcd,lfd->slcf/dot_general | solution.py:369
  259.3 12.9 %fusion.28 = bf16[8,2,40,2048]{3,2,0,1:T(8,128)(2,1)S(1)} fusion(bf16[8,2,40,1408]{3,2,0,1:T(8,128)(2,1)} %get-tuple-element.32, bf16[8,2,40,1408]{3,2,0,1:T(8,128)(2,1)} %get-tuple-element.31, bf16[2,2048,1408]{2,1,0:T(8,128)(2,1)} %param.23, bf16[2,2048,1408]{2,1,0:T(8,128)(2,1)} %param.22), kind=kOutput, calls=%fused_computation.43 | convolution fusion | flops 7436632064 | bytes 29294592 | tf_op jit(solution)/shard_map/slcf,ldf->slcd/dot_general | solution.py:374
  272.7 1.6 pad_maximum_fusion.3
  274.3 5.3 %all-to-all-start.3 = ((bf16[8,72,2048]{2,1,0:T(8,128)(2,1)}), bf16[8,72,2048]{2,1,0:T(8,128)(2,1)}, u32[]{:S(2)}, u32[]{:S(2)}) async-start(bf16[8,72,2048]{2,1,0:T(8,128)(2,1)} %pad_maximum_fusion.3), calls=%async_computation.3 | async-start | bytes 4718592 | tf_op jit(solution)/shard_map/all_to_all | solution.py:241
  279.6 1.8 fusion.95
  282.5 3.7 %multiply_reduce_fusion = (f32[512]{0:T(512)S(1)}, f32[512,2048]{1,0:T(8,128)S(1)}) fusion(bf16[512,2048]{1,0:T(8,128)(2,1)S(1)} %copy-done.25, f32[512,2048]{1,0:T(8,128)S(1)} %fusion.95, f32[512]{0:T(512)S(1)} %bitcast.177, bf16[2048,768]{1,0:T(8,128)(2,1)S(1)} %bitcast.185, f32[512,768]{1,0:T(8,128)} %fusion.97, f32[512,768]{1,0:T(8,128)S(1)} %copy-done.34), kind=kOutput, calls=%fused_computation.17 | convolution fusion | flops 1618214400 | bytes 16781312 | tf_op jit(solution)/shard_map/dot_general | solution.py:18
  286.2 1.4 fusion.99
  288.3 1.8 fusion.98
  290.2 1.9 fusion.51
  292.5 4.2 %add_multiply_fusion = f32[512,2048]{1,0:T(8,128)} fusion(f32[512,2048]{1,0:T(8,128)S(1)} %fusion.51, bf16[2048,768]{1,0:T(8,128)(2,1)S(1)} %bitcast.182, f32[512]{0:T(512)S(1)} %bitcast.178, f32[512,768]{1,0:T(8,128)S(1)} %copy-done.34, f32[512,768]{1,0:T(8,128)S(1)} %fusion.98, f32[512,768]{1,0:T(8,128)S(1)} %copy-done.35), kind=kOutput, calls=%fused_computation.18 | convolution fusion | flops 1616642048 | bytes 16254976 | tf_op jit(solution)/shard_map/dot_general | solution.py:18
  297.6 9.5 %all-to-all-done.3 = bf16[8,72,2048]{2,1,0:T(8,128)(2,1)} async-done(((bf16[8,72,2048]{2,1,0:T(8,128)(2,1)}), bf16[8,72,2048]{2,1,0:T(8,128)(2,1)}, u32[]{:S(2)}, u32[]{:S(2)}) %all-to-all-start.3) | async-done | bytes 2359328 | tf_op jit(solution)/shard_map/all_to_all | solution.py:241
  307.0 5.0 %convolution_add_fusion = f32[512,2048]{1,0:T(8,128)S(1)} fusion(f32[512,2048]{1,0:T(8,128)} %add_multiply_fusion, bf16[512,576]{0,1:T(8,128)(2,1)S(1)} %select_reduce_fusion.1, bf16[576,2048]{1,0:T(8,128)(2,1)} %bitcast.42), kind=kOutput, calls=%fused_computation.42 | convolution fusion | flops 1209008128 | bytes 11337728 | tf_op jit(solution)/shard_map/dot_general | solution.py:160
  312.8 2.0 collective-permute-done.20
  316.4 34.4 %collective-permute-done.18 = bf16[128,2048]{1,0:T(8,128)(2,1)S(1)} collective-permute-done((bf16[128,2048]{1,0:T(8,128)(2,1)S(1)}, bf16[128,2048]{1,0:T(8,128)(2,1)S(1)}, u32[]{:S(2)}, u32[]{:S(2)}) %collective-permute-start.18) | collective-permute-done | bytes 524320 | tf_op jit(solution)/shard_map/ppermute | solution.py:238
  351.7 10.0 %collective-permute-done.21 = bf16[128,2048]{1,0:T(8,128)(2,1)S(1)} collective-permute-done((bf16[128,2048]{1,0:T(8,128)(2,1)S(1)}, bf16[128,2048]{1,0:T(8,128)(2,1)S(1)}, u32[]{:S(2)}, u32[]{:S(2)}) %collective-permute-start.21) | collective-permute-done | bytes 524320 | tf_op jit(solution)/shard_map/ppermute | solution.py:238
  361.7 1.6 fusion.48
  (179 shorter events, 30.0 us)
Async XLA Ops:
  0.6 7.7 %copy-start = (bf16[2048,60]{0,1:T(8,128)(2,1)S(1)}, bf16[2048,60]{0,1:T(8,128)(2,1)}, u32[]{:S(2)}) copy-start(bf16[2048,60]{0,1:T(8,128)(2,1)} %param.17) | copy-start | bytes 737284
  0.6 11.6 %copy-start.17 = (bf16[64,2816]{1,0:T(8,128)(2,1)S(1)}, bf16[64,2816]{1,0:T(8,128)(2,1)}, u32[]{:S(2)}) copy-start(bf16[64,2816]{1,0:T(8,128)(2,1)} %param.20) | copy-start | bytes 1081348
  0.7 12.0 %copy-start.18 = (bf16[2816,64]{0,1:T(8,128)(2,1)S(1)}, bf16[2816,64]{0,1:T(8,128)(2,1)}, u32[]{:S(2)}) copy-start(bf16[2816,64]{0,1:T(8,128)(2,1)} %param.21) | copy-start | bytes 1081348
  0.7 28.0 %collective-permute-start.2 = (bf16[128,2048]{1,0:T(8,128)(2,1)}, bf16[128,2048]{1,0:T(8,128)(2,1)}, u32[]{:S(2)}, u32[]{:S(2)}) collective-permute-start(bf16[128,2048]{1,0:T(8,128)(2,1)} %param.13), channel_id=1, source_target_pairs={{0,16},{1,17},{2,18},{3,19},{4,20},{5,21},{6,22},{7,23},{8,24},{9,... | collective-permute-start | bytes 1572872 | tf_op jit(solution)/shard_map/ppermute | solution.py:238
  10.6 17.9 %collective-permute-start = (f32[128,13]{0,1:T(8,128)S(1)}, f32[128,13]{0,1:T(8,128)S(1)}, u32[]{:S(2)}, u32[]{:S(2)}) collective-permute-start(f32[128,13]{0,1:T(8,128)S(1)} %pad_maximum_fusion.17), channel_id=1, source_target_pairs={{0,16},{1,17},{2,18},{3,19},{4,20},{5,21},{6,22},{7,23},{8,24},{9,... | collective-permute-start | bytes 19976 | tf_op jit(solution)/shard_map/ppermute | solution.py:238
  14.0 16.5 %copy-start.8 = (bf16[128,2048]{1,0:T(8,128)(2,1)S(1)}, bf16[128,2048]{1,0:T(8,128)(2,1)}, u32[]{:S(2)}) copy-start(bf16[128,2048]{1,0:T(8,128)(2,1)} %param.14) | copy-start | bytes 1572868
  14.9 18.4 %collective-permute-start.4 = (bf16[2,3,64,768]{3,2,1,0:T(8,128)(2,1)}, bf16[2,3,64,768]{3,2,1,0:T(8,128)(2,1)}, u32[]{:S(2)}, u32[]{:S(2)}) collective-permute-start(bf16[2,3,64,768]{3,2,1,0:T(8,128)(2,1)} %get-tuple-element.41), channel_id=1, source_target_pairs={{0,1},{1,0},{2,3},{3,2},{4,5},{5,4},{6,7},{7,6},{8,9},{9,8},{10,11... | collective-permute-start | bytes 1769480 | tf_op jit(solution)/shard_map/ppermute | solution.py:238
  28.5 1.8 collective-permute-start.1
  29.8 26.9 %collective-permute-start.3 = (bf16[256,2048]{1,0:T(8,128)(2,1)S(1)}, bf16[256,2048]{1,0:T(8,128)(2,1)S(1)}, u32[]{:S(2)}, u32[]{:S(2)}) collective-permute-start(bf16[256,2048]{1,0:T(8,128)(2,1)S(1)} %pad_maximum_fusion.10), channel_id=1, source_target_pairs={{0,1},{1,0},{2,3},{3,2},{4,5},{5,4},{6,7},{7,6},{8,9},{9,8},{10,11... | collective-permute-start | bytes 3145736 | tf_op jit(solution)/shard_map/ppermute | solution.py:238
  30.4 26.2 %collective-permute-start.10 = (bf16[128,2048]{1,0:T(8,128)(2,1)S(1)}, bf16[128,2048]{1,0:T(8,128)(2,1)S(1)}, u32[]{:S(2)}, u32[]{:S(2)}) collective-permute-start(bf16[128,2048]{1,0:T(8,128)(2,1)S(1)} %copy-done.8), channel_id=1, source_target_pairs={{0,16},{1,17},{2,18},{3,19},{4,20},{5,21},{6,22},{7,23},{8,24},{9,... | collective-permute-start | bytes 1572872 | tf_op jit(solution)/shard_map/ppermute | solution.py:238
  31.2 25.5 %copy-start.15 = (bf16[576,512]{1,0:T(8,128)(2,1)}, bf16[576,512]{1,0:T(8,128)(2,1)S(1)}, u32[]{:S(2)}) copy-start(bf16[576,512]{1,0:T(8,128)(2,1)S(1)} %convert_reduce_fusion) | copy-start | bytes 1769476
  33.3 23.3 %copy-start.21 = (bf16[512,2048]{1,0:T(8,128)(2,1)S(1)}, bf16[512,2048]{1,0:T(8,128)(2,1)}, u32[]{:S(2)}) copy-start(bf16[512,2048]{1,0:T(8,128)(2,1)} %constant_dynamic-update-slice_fusion.1) | copy-start | bytes 6291460
  36.0 49.5 %collective-permute-start.5 = (bf16[3,128,768]{2,1,0:T(8,128)(2,1)S(1)}, bf16[3,128,768]{2,1,0:T(8,128)(2,1)}, u32[]{:S(2)}, u32[]{:S(2)}) collective-permute-start(bf16[3,128,768]{2,1,0:T(8,128)(2,1)S(1)} %bitcast.166), channel_id=1, source_target_pairs={{0,8},{1,9},{2,10},{3,11},{4,12},{5,13},{6,14},{7,15},{8,0},{9,1},... | collective-permute-start | bytes 1769480 | tf_op jit(solution)/shard_map/ppermute | solution.py:238
  56.6 27.7 %collective-permute-start.11 = (bf16[3,128,768]{2,1,0:T(8,128)(2,1)}, bf16[3,128,768]{2,1,0:T(8,128)(2,1)}, u32[]{:S(2)}, u32[]{:S(2)}) collective-permute-start(bf16[3,128,768]{2,1,0:T(8,128)(2,1)} %get-tuple-element.16), channel_id=1, source_target_pairs={{0,16},{1,17},{2,18},{3,19},{4,20},{5,21},{6,22},{7,23},{8,24},{9,... | collective-permute-start | bytes 1769480 | tf_op jit(solution)/shard_map/ppermute | solution.py:238
  59.6 24.8 %copy-start.29 = (s32[16]{0:T(128)S(1)}, s32[16]{0:T(128)}, u32[]{:S(2)}) copy-start(s32[16]{0:T(128)} %constant.164.clone) | copy-start | bytes 196
  59.6 143.8 %all-to-all-start = ((bf16[8,72,2048]{2,1,0:T(8,128)(2,1)}), bf16[8,72,2048]{2,1,0:T(8,128)(2,1)S(1)}, u32[]{:S(2)}, u32[]{:S(2)}) async-start(bf16[8,72,2048]{2,1,0:T(8,128)(2,1)} %bitcast.164), calls=%async_computation | async-start | bytes 4718592 | tf_op jit(solution)/shard_map/all_to_all | solution.py:241
  84.4 33.4 %collective-permute-start.12 = (bf16[3,128,768]{2,1,0:T(8,128)(2,1)}, bf16[3,128,768]{2,1,0:T(8,128)(2,1)S(1)}, u32[]{:S(2)}, u32[]{:S(2)}) collective-permute-start(bf16[3,128,768]{2,1,0:T(8,128)(2,1)} %collective-permute-done.11), channel_id=1, source_target_pairs={{0,8},{1,9},{2,10},{3,11},{4,12},{5,13},{6,14},{7,15},{8,0},{9,1},... | collective-permute-start | bytes 1769480 | tf_op jit(solution)/shard_map/ppermute | solution.py:238
  85.5 35.5 %copy-start.28 = (bf16[2048]{0:T(1024)(128)(2,1)S(1)}, bf16[2048]{0:T(1024)(128)(2,1)}, u32[]{:S(2)}) copy-start(bf16[2048]{0:T(1024)(128)(2,1)} %param.18) | copy-start | bytes 12292
  85.5 37.6 %copy-start.9 = (bf16[128,2048]{1,0:T(8,128)(2,1)S(1)}, bf16[128,2048]{1,0:T(8,128)(2,1)}, u32[]{:S(2)}) copy-start(bf16[128,2048]{1,0:T(8,128)(2,1)} %param.14) | copy-start | bytes 1572868
  85.5 37.6 %copy-start.11 = (bf16[128,2048]{1,0:T(8,128)(2,1)S(1)}, bf16[128,2048]{1,0:T(8,128)(2,1)}, u32[]{:S(2)}) copy-start(bf16[128,2048]{1,0:T(8,128)(2,1)} %copy-done.10) | copy-start | bytes 1572868
  86.7 36.5 %collective-permute-start.6 = (bf16[2,3,64,768]{3,2,1,0:T(8,128)(2,1)S(1)}, bf16[2,3,64,768]{3,2,1,0:T(8,128)(2,1)S(1)}, u32[]{:S(2)}, u32[]{:S(2)}) collective-permute-start(bf16[2,3,64,768]{3,2,1,0:T(8,128)(2,1)S(1)} %get-tuple-element.39), channel_id=1, source_target_pairs={{0,2},{1,3},{2,0},{3,1},{4,6},{5,7},{6,4},{7,5},{8,10},{9,11},{10,... | collective-permute-start | bytes 1769480 | tf_op jit(solution)/shard_map/ppermute | solution.py:238
  88.3 35.6 %collective-permute-start.8 = (bf16[2,3,64,768]{3,2,1,0:T(8,128)(2,1)S(1)}, bf16[2,3,64,768]{3,2,1,0:T(8,128)(2,1)S(1)}, u32[]{:S(2)}, u32[]{:S(2)}) collective-permute-start(bf16[2,3,64,768]{3,2,1,0:T(8,128)(2,1)S(1)} %get-tuple-element.38), channel_id=1, source_target_pairs={{0,4},{1,5},{2,6},{3,7},{4,0},{5,1},{6,2},{7,3},{8,12},{9,13},{10,... | collective-permute-start | bytes 1769480 | tf_op jit(solution)/shard_map/ppermute | solution.py:238
  118.9 16.3 %collective-permute-start.13 = (bf16[2,3,64,768]{3,2,1,0:T(8,128)(2,1)S(1)}, bf16[2,3,64,768]{3,2,1,0:T(8,128)(2,1)S(1)}, u32[]{:S(2)}, u32[]{:S(2)}) collective-permute-start(bf16[2,3,64,768]{3,2,1,0:T(8,128)(2,1)S(1)} %get-tuple-element.35), channel_id=1, source_target_pairs={{0,2},{1,3},{2,0},{3,1},{4,6},{5,7},{6,4},{7,5},{8,10},{9,11},{10,... | collective-permute-start | bytes 1769480 | tf_op jit(solution)/shard_map/ppermute | solution.py:238
  121.5 16.2 %collective-permute-start.15 = (bf16[2,3,64,768]{3,2,1,0:T(8,128)(2,1)S(1)}, bf16[2,3,64,768]{3,2,1,0:T(8,128)(2,1)S(1)}, u32[]{:S(2)}, u32[]{:S(2)}) collective-permute-start(bf16[2,3,64,768]{3,2,1,0:T(8,128)(2,1)S(1)} %get-tuple-element.34), channel_id=1, source_target_pairs={{0,4},{1,5},{2,6},{3,7},{4,0},{5,1},{6,2},{7,3},{8,12},{9,13},{10,... | collective-permute-start | bytes 1769480 | tf_op jit(solution)/shard_map/ppermute | solution.py:238
  123.2 16.2 %collective-permute-start.19 = (bf16[256,2048]{1,0:T(8,128)(2,1)S(1)}, bf16[256,2048]{1,0:T(8,128)(2,1)S(1)}, u32[]{:S(2)}, u32[]{:S(2)}) collective-permute-start(bf16[256,2048]{1,0:T(8,128)(2,1)S(1)} %pad_maximum_fusion.11), channel_id=1, source_target_pairs={{0,1},{1,0},{2,3},{3,2},{4,5},{5,4},{6,7},{7,6},{8,9},{9,8},{10,11... | collective-permute-start | bytes 3145736 | tf_op jit(solution)/shard_map/ppermute | solution.py:238
  123.4 11.8 %copy-start.2 = (bf16[4,3,64,768]{3,2,1,0:T(8,128)(2,1)}, bf16[4,3,64,768]{3,2,1,0:T(8,128)(2,1)S(1)}, u32[]{:S(2)}) copy-start(bf16[4,3,64,768]{3,2,1,0:T(8,128)(2,1)S(1)} %pad_maximum_fusion.6.refs_0_) | copy-start | bytes 3538948
  123.4 39.6 %collective-permute-start.7 = (bf16[4,3,64,768]{3,2,1,0:T(8,128)(2,1)S(1)}, bf16[4,3,64,768]{3,2,1,0:T(8,128)(2,1)S(1)}, u32[]{:S(2)}, u32[]{:S(2)}) collective-permute-start(bf16[4,3,64,768]{3,2,1,0:T(8,128)(2,1)S(1)} %pad_maximum_fusion.6.refs_0_), channel_id=1, source_target_pairs={{0,4},{1,5},{2,6},{3,7},{4,0},{5,1},{6,2},{7,3},{8,12},{9,13},{10,... | collective-permute-start | bytes 3538952 | tf_op jit(solution)/shard_map/ppermute | solution.py:238
  124.1 13.8 %copy-start.3 = (bf16[4,3,64,768]{3,2,1,0:T(8,128)(2,1)}, bf16[4,3,64,768]{3,2,1,0:T(8,128)(2,1)S(1)}, u32[]{:S(2)}) copy-start(bf16[4,3,64,768]{3,2,1,0:T(8,128)(2,1)S(1)} %pad_maximum_fusion.7.refs_2_) | copy-start | bytes 3538948
  124.1 39.0 %collective-permute-start.9 = (bf16[4,3,64,768]{3,2,1,0:T(8,128)(2,1)S(1)}, bf16[4,3,64,768]{3,2,1,0:T(8,128)(2,1)S(1)}, u32[]{:S(2)}, u32[]{:S(2)}) collective-permute-start(bf16[4,3,64,768]{3,2,1,0:T(8,128)(2,1)S(1)} %pad_maximum_fusion.7.refs_2_), channel_id=1, source_target_pairs={{0,2},{1,3},{2,0},{3,1},{4,6},{5,7},{6,4},{7,5},{8,10},{9,11},{10,... | collective-permute-start | bytes 3538952 | tf_op jit(solution)/shard_map/ppermute | solution.py:238
  135.3 50.4 %collective-permute-start.14 = (bf16[4,3,64,768]{3,2,1,0:T(8,128)(2,1)S(1)}, bf16[4,3,64,768]{3,2,1,0:T(8,128)(2,1)S(1)}, u32[]{:S(2)}, u32[]{:S(2)}) collective-permute-start(bf16[4,3,64,768]{3,2,1,0:T(8,128)(2,1)S(1)} %pad_maximum_fusion.8.refs_4_), channel_id=1, source_target_pairs={{0,4},{1,5},{2,6},{3,7},{4,0},{5,1},{6,2},{7,3},{8,12},{9,13},{10,... | collective-permute-start | bytes 3538952 | tf_op jit(solution)/shard_map/ppermute | solution.py:238
  137.9 48.8 %collective-permute-start.16 = (bf16[4,3,64,768]{3,2,1,0:T(8,128)(2,1)S(1)}, bf16[4,3,64,768]{3,2,1,0:T(8,128)(2,1)}, u32[]{:S(2)}, u32[]{:S(2)}) collective-permute-start(bf16[4,3,64,768]{3,2,1,0:T(8,128)(2,1)S(1)} %pad_maximum_fusion.9.refs_6_), channel_id=1, source_target_pairs={{0,2},{1,3},{2,0},{3,1},{4,6},{5,7},{6,4},{7,5},{8,10},{9,11},{10,... | collective-permute-start | bytes 3538952 | tf_op jit(solution)/shard_map/ppermute | solution.py:238
  163.0 22.6 %copy-start.12 = (bf16[4,3,64,768]{3,2,1,0:T(8,128)(2,1)}, bf16[4,3,64,768]{3,2,1,0:T(8,128)(2,1)S(1)}, u32[]{:S(2)}) copy-start(bf16[4,3,64,768]{3,2,1,0:T(8,128)(2,1)S(1)} %collective-permute-done.7.refs_1_) | copy-start | bytes 3538948
  163.0 22.6 %copy-start.13 = (bf16[4,3,64,768]{3,2,1,0:T(8,128)(2,1)}, bf16[4,3,64,768]{3,2,1,0:T(8,128)(2,1)S(1)}, u32[]{:S(2)}) copy-start(bf16[4,3,64,768]{3,2,1,0:T(8,128)(2,1)S(1)} %collective-permute-done.9.refs_3_) | copy-start | bytes 3538948
  203.4 32.7 %all-to-all-start.2 = ((bf16[8,72,2048]{2,1,0:T(8,128)(2,1)}), bf16[8,72,2048]{2,1,0:T(8,128)(2,1)}, u32[]{:S(2)}, u32[]{:S(2)}) async-start(bf16[8,72,2048]{2,1,0:T(8,128)(2,1)} %bitcast.165), calls=%async_computation.2 | async-start | bytes 4718592 | tf_op jit(solution)/shard_map/all_to_all | solution.py:241
  208.5 20.9 %slice-start = ((s8[11534336]{0:T(1024)(128)(4,1)}), s8[4194304]{0:T(1024)(128)(4,1)S(1)}, s32[]{:S(2)}) async-start(s8[11534336]{0:T(1024)(128)(4,1)} %bitcast.179), calls=%async_computation.4 | async-start | bytes 8388608
  217.6 11.7 %slice-start.1 = ((s8[11534336]{0:T(1024)(128)(4,1)}), s8[4194304]{0:T(1024)(128)(4,1)S(1)}, s32[]{:S(2)}) async-start(s8[11534336]{0:T(1024)(128)(4,1)} %bitcast.179), calls=%async_computation.5 | async-start | bytes 8388608
  217.6 11.8 %slice-start.2 = ((s8[11534336]{0:T(1024)(128)(4,1)}), s8[3145728]{0:T(1024)(128)(4,1)S(1)}, s32[]{:S(2)}) async-start(s8[11534336]{0:T(1024)(128)(4,1)} %bitcast.179), calls=%async_computation.6 | async-start | bytes 6291456
  236.0 38.2 %all-to-all-start.1 = ((bf16[8,72,2048]{2,1,0:T(8,128)(2,1)}), bf16[8,72,2048]{2,1,0:T(8,128)(2,1)S(1)}, u32[]{:S(2)}, u32[]{:S(2)}) async-start(bf16[8,72,2048]{2,1,0:T(8,128)(2,1)} %pad_maximum_fusion.2), calls=%async_computation.1 | async-start | bytes 4718592 | tf_op jit(solution)/shard_map/all_to_all | solution.py:241
  274.3 32.8 %all-to-all-start.3 = ((bf16[8,72,2048]{2,1,0:T(8,128)(2,1)}), bf16[8,72,2048]{2,1,0:T(8,128)(2,1)}, u32[]{:S(2)}, u32[]{:S(2)}) async-start(bf16[8,72,2048]{2,1,0:T(8,128)(2,1)} %pad_maximum_fusion.3), calls=%async_computation.3 | async-start | bytes 4718592 | tf_op jit(solution)/shard_map/all_to_all | solution.py:241
  286.2 10.5 %copy-start.6 = (f32[512,2048]{1,0:T(8,128)}, f32[512,2048]{1,0:T(8,128)S(1)}, u32[]{:S(2)}) copy-start(f32[512,2048]{1,0:T(8,128)S(1)} %get-tuple-element.30) | copy-start | bytes 12582916
  288.2 9.2 %collective-permute-start.22 = (f32[256,5]{0,1:T(8,128)S(1)}, f32[256,5]{0,1:T(8,128)S(1)}, u32[]{:S(2)}, u32[]{:S(2)}) collective-permute-start(f32[256,5]{0,1:T(8,128)S(1)} %pad_maximum_fusion.16), channel_id=1, source_target_pairs={{0,1},{1,0},{2,3},{3,2},{4,5},{5,4},{6,7},{7,6},{8,9},{9,8},{10,11... | collective-permute-start | bytes 15368 | tf_op jit(solution)/shard_map/ppermute | solution.py:238
  296.9 15.4 %collective-permute-start.17 = (bf16[256,2048]{1,0:T(8,128)(2,1)S(1)}, bf16[256,2048]{1,0:T(8,128)(2,1)S(1)}, u32[]{:S(2)}, u32[]{:S(2)}) collective-permute-start(bf16[256,2048]{1,0:T(8,128)(2,1)S(1)} %slice.221), channel_id=1, source_target_pairs={{0,1},{1,0},{2,3},{3,2},{4,5},{5,4},{6,7},{7,6},{8,9},{9,8},{10,11... | collective-permute-start | bytes 3145736 | tf_op jit(solution)/shard_map/ppermute | solution.py:238
  297.5 14.8 %collective-permute-start.23 = (f32[128,5]{0,1:T(8,128)S(1)}, f32[128,5]{0,1:T(8,128)S(1)}, u32[]{:S(2)}, u32[]{:S(2)}) collective-permute-start(f32[128,5]{0,1:T(8,128)S(1)} %slice.160), channel_id=1, source_target_pairs={{0,16},{1,17},{2,18},{3,19},{4,20},{5,21},{6,22},{7,23},{8,24},{9,... | collective-permute-start | bytes 7688 | tf_op jit(solution)/shard_map/ppermute | solution.py:238
  312.2 2.7 collective-permute-start.20
  312.8 38.0 %collective-permute-start.18 = (bf16[128,2048]{1,0:T(8,128)(2,1)S(1)}, bf16[128,2048]{1,0:T(8,128)(2,1)S(1)}, u32[]{:S(2)}, u32[]{:S(2)}) collective-permute-start(bf16[128,2048]{1,0:T(8,128)(2,1)S(1)} %slice.223), channel_id=1, source_target_pairs={{0,16},{1,17},{2,18},{3,19},{4,20},{5,21},{6,22},{7,23},{8,24},{9,... | collective-permute-start | bytes 1572872 | tf_op jit(solution)/shard_map/ppermute | solution.py:238
  315.2 46.5 %copy-start.20 = (f32[128,60]{0,1:T(8,128)S(1)}, f32[128,60]{0,1:T(8,128)}, u32[]{:S(2)}) copy-start(f32[128,60]{0,1:T(8,128)} %copy-done.19) | copy-start | bytes 92164
  315.2 46.5 %copy-start.26 = (f32[2048]{0:T(1024)S(1)}, f32[2048]{0:T(1024)}, u32[]{:S(2)}) copy-start(f32[2048]{0:T(1024)} %convert_element_type.118) | copy-start | bytes 24580
  315.3 46.4 %collective-permute-start.21 = (bf16[128,2048]{1,0:T(8,128)(2,1)S(1)}, bf16[128,2048]{1,0:T(8,128)(2,1)S(1)}, u32[]{:S(2)}, u32[]{:S(2)}) collective-permute-start(bf16[128,2048]{1,0:T(8,128)(2,1)S(1)} %slice.222), channel_id=1, source_target_pairs={{0,16},{1,17},{2,18},{3,19},{4,20},{5,21},{6,22},{7,23},{8,24},{9,... | collective-permute-start | bytes 1572872 | tf_op jit(solution)/shard_map/ppermute | solution.py:238
  (19 other events, 55.6 us)
